TPU v7x, 128 devices: a whole 4x4x4 slice. The times are simulated.
128 devices in a mesh: grp: 4 (over z_lo, core), dp: 32 (over z_hi, y, x).
Axes of the slice: x: 4, y: 4, z: 4 (z_hi: 2, z_lo: 2; z = z_hi * 2 + z_lo), core: 2. Of those that a mesh axis runs over, the one named last changes fastest.
Arguments:
- activations: bfloat16 [262144, 1280], P(('grp', 'dp')), may hold values from -6 to 6
- cotangent: bfloat16 [262144, 1280], P(('grp', 'dp')), may hold values from -0.01171875 to 0.01171875
- carried_error: float32 [128, 1280, 1280], P(('grp', 'dp')), may hold values from -6 to 6
- owner_error: float32 [1280, 1280], P(('grp', 'dp')), may hold values from -6 to 6
Outputs:
- update: float32 [1280, 1280], replicated
All inputs are finite; a program needn't handle non-finite values.
Results may differ from a plain program's by a relative error of at most 0.012.
Values may be sent and summed in bfloat16 or wider, within the bound.
No kernel may reach another device: no remote copies, remote signals or barrier semaphores. Data moves between devices by JAX's collectives and lax.ppermute only.
A program may use at most 128 MiB of HBM per device.

v0:
```python
import jax
import jax.numpy as jnp
from jax import lax
from jax.sharding import PartitionSpec as P

D = 1280
BLOCK = 128


def cut_along(value, dim, devices):
    shape = value.shape
    parts = value.reshape(*shape[:dim], devices, shape[dim] // devices, *shape[dim + 1 :])
    return jnp.moveaxis(parts, dim, 0)


def sent_and_summed(value, axis, dim):
    devices = lax.axis_size(axis)
    parts = lax.all_to_all(cut_along(value, dim, devices), axis, 0, 0, tiled=True)
    return jnp.sum(parts, axis=0)


def side_by_side(arrays, axis, dim, along):
    ends, at = ([], 0)
    for a in arrays[:-1]:
        at += a.shape[along]
        ends.append(at)
    both = jnp.concatenate(arrays, axis=along)
    return tuple(jnp.split(lax.all_gather(both, axis, axis=dim, tiled=True), ends, axis=along))


def quantize(values):
    blocks = values.reshape(values.shape[:-1] + (values.shape[-1] // BLOCK, BLOCK))
    largest = jnp.max(jnp.abs(blocks), axis=-1)
    scales = ((largest + 1e-06) / 127.0).astype(jnp.bfloat16)
    levels = (blocks / scales.astype(jnp.float32)[..., None]).astype(jnp.bfloat16)
    return (levels.reshape(values.shape), scales)


def dequantize(levels, scales):
    blocks = levels.reshape(levels.shape[:-1] + (levels.shape[-1] // BLOCK, BLOCK)).astype(
        jnp.float32
    )
    return (blocks * scales.astype(jnp.float32)[..., None]).reshape(levels.shape)


def on_device(activations, cotangent, carried_error, owner_error):
    gradient = lax.dot_general(
        activations, cotangent, (((0,), (0,)), ((), ())), preferred_element_type=jnp.float32
    )
    levels, scales = quantize(gradient + carried_error[0])
    grp_count = lax.axis_size("grp")
    dp_count = lax.axis_size("dp")
    owner_rows = D // (grp_count * dp_count)
    block_count = D // BLOCK
    got_levels, got_scales = (
        lax.all_to_all(
            levels.reshape(grp_count, dp_count, owner_rows, D),
            "dp",
            split_axis=1,
            concat_axis=1,
            tiled=True,
        ),
        lax.all_to_all(
            scales.reshape(grp_count, dp_count, owner_rows, block_count),
            "dp",
            split_axis=1,
            concat_axis=1,
            tiled=True,
        ),
    )
    partial_value = jnp.sum(dequantize(got_levels, got_scales), axis=1)
    summed = sent_and_summed(partial_value, "grp", 0)[0]
    summed = summed + owner_error
    owner_level, owner_scale = quantize(summed)
    all_levels, all_scales = side_by_side((owner_level, owner_scale), ("grp", "dp"), 0, 1)
    return dequantize(all_levels, all_scales)


def solution(mesh):
    return jax.shard_map(
        on_device,
        mesh=mesh,
        in_specs=(
            P(("grp", "dp"), None),
            P(("grp", "dp"), None),
            P(("grp", "dp"), None, None),
            P(("grp", "dp"), None),
        ),
        out_specs=P(),
        check_vma=False,
    )
```

profile of v0, /device:TPU:1, one launch (start us, length us, event | category | flops | bytes accessed | tf_op | source)
XLA Modules:
  0.0 499.8 jit_solution(17454378079995790397)
XLA Ops:
  6.5 14.4 %fusion.1 = (f32[1280,1280]{1,0:T(8,128)}, f32[1280,1280]{1,0:T(8,128)}) fusion(f32[1,1280,1280]{2,1,0:T(8,128)} %param.6, bf16[2048,1280]{1,0:T(8,128)(2,1)} %param.4, bf16[2048,1280]{1,0:T(8,128)(2,1)} %param.5), kind=kOutput, calls=%fused_computation.9 | convolution fusion | flops 6714163200 | bytes 30146560 | tf_op jit(solution)/shard_map/dot_general | solution.py:47
  21.0 8.2 %copy.38 = f32[1280,1280]{0,1:T(8,128)} copy(f32[1280,1280]{1,0:T(8,128)} %get-tuple-element.7) | data formatting | bytes 13107200 | tf_op jit(solution)/shard_map/abs | solution.py:33
  29.1 3.3 reduce_max.18
  32.4 0.7 convert_element_type.58
  33.1 0.2 copy.55
  33.3 0.9 reshape.46
  34.2 11.4 %all-to-all-start.1 = ((bf16[32,2,200]{2,1,0:T(2,128)(2,1)}), bf16[32,2,200]{2,1,0:T(2,128)(2,1)S(1)}, u32[]{:S(2)}, u32[]{:S(2)}) async-start(bf16[32,2,200]{2,1,0:T(2,128)(2,1)} %reshape.46), calls=%async_computation.1 | async-start | bytes 65536 | tf_op jit(solution)/shard_map/all_to_all | solution.py:63
  45.6 0.2 copy.39
  45.8 8.1 %div.36 = f32[1280,10,128]{2,1,0:T(8,128)} broadcast(f32[1280,10]{1,0:T(8,128)S(1)} %copy.39), dimensions={0,1} | broadcast | bytes 6604800 | tf_op jit(solution)/shard_map/div | solution.py:35
  53.9 11.4 %div.37 = f32[4,32,10,1280]{3,2,1,0:T(8,128)} reshape(f32[1280,10,128]{2,1,0:T(8,128)} %div.36) | data formatting | bytes 13107200 | tf_op jit(solution)/shard_map/div | solution.py:35
  65.3 8.6 %reshape.42 = f32[4,32,10,1280]{3,2,1,0:T(8,128)} reshape(f32[1280,1280]{1,0:T(8,128)} %get-tuple-element.8) | data formatting | bytes 13107200 | tf_op jit(solution)/shard_map/reshape | solution.py:32
  74.0 11.4 %divide_convert_fusion = bf16[4,32,10,1280]{3,2,1,0:T(8,128)(2,1)} fusion(f32[4,32,10,1280]{3,2,1,0:T(8,128)} %reshape.42, f32[4,32,10,1280]{3,2,1,0:T(8,128)} %div.37), kind=kLoop, calls=%fused_computation | loop fusion | flops 3276800 | bytes 16384000 | tf_op jit(solution)/shard_map/convert_element_type | solution.py:35
  85.3 6.8 %copy.40 = bf16[4,32,10,1280]{3,0,2,1:T(4,128)(2,1)} copy(bf16[4,32,10,1280]{3,2,1,0:T(8,128)(2,1)} %divide_convert_fusion) | data formatting | bytes 6553600 | tf_op jit(solution)/shard_map/convert_element_type | solution.py:35
  92.1 0.0 all-to-all-done.1
  92.1 9.1 %all-to-all-start = ((bf16[4,32,10,1280]{3,0,2,1:T(4,128)(2,1)}), bf16[4,32,10,1280]{3,0,2,1:T(4,128)(2,1)S(1)}, u32[]{:S(2)}, u32[]{:S(2)}) async-start(bf16[4,32,10,1280]{3,0,2,1:T(4,128)(2,1)} %copy.40), calls=%async_computation | async-start | bytes 6553600 | tf_op jit(solution)/shard_map/all_to_all | solution.py:56
  101.2 0.0 all-gather.3.cloned.1.call-start
  101.3 1.0 reshape.47
  102.3 1.3 copy.43
  103.6 1.2 copy.44
  104.8 6.8 %mul.22 = f32[4,32,10,10,128]{4,3,1,2,0:T(8,128)} broadcast(f32[4,32,10,10]{3,1,2,0:T(8,128)} %copy.44), dimensions={0,1,2,3} | broadcast | bytes 6604800 | tf_op jit(solution)/shard_map/mul | solution.py:43
  111.5 9.1 %mul.23 = f32[4,32,10,1280]{3,1,2,0:T(8,128)} reshape(f32[4,32,10,10,128]{4,3,1,2,0:T(8,128)} %mul.22) | data formatting | bytes 13107200 | tf_op jit(solution)/shard_map/mul | solution.py:43
  120.6 0.0 copy-start
  120.7 20.9 %all-to-all-done = bf16[4,32,10,1280]{3,0,2,1:T(4,128)(2,1)S(1)} async-done(((bf16[4,32,10,1280]{3,0,2,1:T(4,128)(2,1)}), bf16[4,32,10,1280]{3,0,2,1:T(4,128)(2,1)S(1)}, u32[]{:S(2)}, u32[]{:S(2)}) %all-to-all-start) | async-done | bytes 3276832 | tf_op jit(solution)/shard_map/all_to_all | solution.py:56
  141.6 4.4 multiply_reduce_fusion
  146.0 0.2 copy.46
  146.2 10.1 %all_to_all.15 = f32[4,1,10,1280]{3,1,2,0:T(1,128)S(1)} all-to-all(f32[4,1,10,1280]{3,1,2,0:T(1,128)S(1)} %copy.46), channel_id=1, replica_groups=mesh['grp'=4,'dp'=32] {'grp'}, dimensions={0} | all-to-all | bytes 409600 | tf_op jit(solution)/shard_map/all_to_all | solution.py:18
  156.4 0.2 reduce_sum.19
  156.6 0.0 copy-done
  156.6 0.1 reduce_max.19
  156.7 0.1 div.41
  156.9 0.6 maximum_bitcast_fusion
  157.5 0.0 all-gather.3.cloned.1.call-update
  157.6 307.8 %all-gather.3.cloned.1.call-done = bf16[128,10,1290]{2,1,0:T(8,128)(2,1)} async-done(((bf16[1,10,1290]{2,1,0:T(8,128)(2,1)}), bf16[128,10,1290]{2,1,0:T(8,128)(2,1)}) %all-gather.3.cloned.1.call-update) | async-done | bytes 3302416 | tf_op jit(solution)/shard_map/all_gather | solution.py:28
  465.4 7.7 %reshape.45 = bf16[1280,1290]{1,0:T(8,128)(2,1)} reshape(bf16[128,10,1290]{2,1,0:T(8,128)(2,1)} %all-gather.3.cloned.1.call-done) | data formatting | bytes 6604800
  473.1 1.0 split.9
  474.1 0.2 copy.51
  474.2 3.3 mul.25
  477.5 8.2 %copy.48 = f32[1280,1280]{1,0:T(8,128)} copy(f32[1280,1280]{0,1:T(8,128)} %bitcast.21) | data formatting | bytes 13107200 | tf_op jit(solution)/shard_map/mul | solution.py:43
  485.7 7.2 %convert_multiply_fusion = f32[1280,1280]{1,0:T(8,128)} fusion(f32[1280,1280]{1,0:T(8,128)} %copy.48, bf16[1280,1290]{1,0:T(8,128)(2,1)} %reshape.45), kind=kLoop, calls=%fused_computation.2 | loop fusion | flops 3276800 | bytes 16384000 | tf_op jit(solution)/shard_map/mul | solution.py:43
  (7 shorter events, 0.1 us)
Async XLA Ops:
  34.2 57.9 %all-to-all-start.1 = ((bf16[32,2,200]{2,1,0:T(2,128)(2,1)}), bf16[32,2,200]{2,1,0:T(2,128)(2,1)S(1)}, u32[]{:S(2)}, u32[]{:S(2)}) async-start(bf16[32,2,200]{2,1,0:T(2,128)(2,1)} %reshape.46), calls=%async_computation.1 | async-start | bytes 65536 | tf_op jit(solution)/shard_map/all_to_all | solution.py:63
  92.1 49.4 %all-to-all-start = ((bf16[4,32,10,1280]{3,0,2,1:T(4,128)(2,1)}), bf16[4,32,10,1280]{3,0,2,1:T(4,128)(2,1)S(1)}, u32[]{:S(2)}, u32[]{:S(2)}) async-start(bf16[4,32,10,1280]{3,0,2,1:T(4,128)(2,1)} %copy.40), calls=%async_computation | async-start | bytes 6553600 | tf_op jit(solution)/shard_map/all_to_all | solution.py:56
  101.2 364.1 %all-gather.3.cloned.1.call-start = ((), (), s32[]{:S(2)}) async-start(), calls=%async_computation.3 | async-start | bytes 5812224 | tf_op jit(solution)/shard_map/all_gather | solution.py:28
  120.6 35.9 %copy-start = (f32[10,1280]{1,0:T(8,128)S(1)}, f32[10,1280]{1,0:T(8,128)}, u32[]{:S(2)}) copy-start(f32[10,1280]{1,0:T(8,128)} %param.7) | copy-start | bytes 153604
Sparse Core Ops, SparseCore 0:
  157.7 307.6 all-gather.2
where the time goes:
time: 501 us; the launch traced here: 500 us
  waiting for transfers between devices  329 us (66%)
  local copies, waits for them, and re-layouts  85.1 us (17%)
  other arithmetic  27.3 us (5%)
  starting transfers between devices  20.5 us (4%)
  matrix products  14.4 us (3%)
  between operations  13.5 us (3%)
  blocking collectives  10.1 us (2%)
    all_gather x1, waiting for transfers between devices, side_by_side(): lax.all_gather(both, axis, axis=dim, tiled=True)  308 us
    mul x4, local copies, waits for them, and re-layouts, dequantize(): blocks * scales.astype(jnp.float32)[..., None]  27.3 us
    all_to_all x1, waiting for transfers between devices, on_device(): lax.all_to_all(levels.reshape(grp_count, dp_count, owner_rows, D), 'dp',...  20.9 us
    div x3, local copies, waits for them, and re-layouts, quantize(): blocks / scales.astype(jnp.float32)[..., None]  19.6 us
    dot_general x1, matrix products, on_device(): lax.dot_general(activations, cotangent, (((0,), (0,)), ((), ())), preferr...  14.4 us
    convert_element_type x2, other arithmetic, quantize(): (blocks / scales.astype(jnp.float32)[..., None]).astype(jnp.bfloat16)  11.4 us
    all_to_all x1, starting transfers between devices, on_device(): lax.all_to_all(scales.reshape(grp_count, dp_count, owner_rows, block_coun...  11.4 us
    all_to_all x1, blocking collectives, sent_and_summed(): lax.all_to_all(cut_along(value, dim, devices), axis, 0, 0, tiled=True)  10.1 us
  transfers between devices with their start and end apart: 3, of which 2 were waited for; matrix products, arithmetic and copies ran while one was open for 13% of the time, Pallas kernels for 0%

commit v1 on v0

v1 whole, which is shorter than its diff:
```python
import functools

import jax
import jax.numpy as jnp
from jax import lax
from jax.experimental import pallas as pl
from jax.experimental.pallas import tpu as pltpu
from jax.sharding import Mesh
from jax.sharding import PartitionSpec as P

D = 1280
BLOCK = 128
HALF = D // 2
COLS = D // BLOCK
AXES = ("zl", "c", "zh", "y", "x")
CHIPS = ("zl", "zh", "y", "x")
N_CHIPS = 64
TILES = HALF // 8 * COLS
PER_CHIP = -(-TILES // N_CHIPS)
OWNED = PER_CHIP * 8
STEP = 128


def quantized(v):
    largest = jnp.max(jnp.abs(v), axis=-1, keepdims=True)
    scale = ((largest + 1e-06) / 127.0).astype(jnp.bfloat16).astype(jnp.float32)
    level = (v * (1.0 / scale)).astype(jnp.bfloat16).astype(jnp.float32)
    return level * scale


def gradient_kernel(where, act, cot, err, window, out, acc):
    acc[...] = lax.dot_general(
        act[...], cot[...], (((0,), (0,)), ((), ())), preferred_element_type=jnp.float32
    )
    for b in range(COLS):
        at = slice(b * BLOCK, (b + 1) * BLOCK)
        acc[:, at] = quantized(acc[:, at] + err[:, at])
    first = (where[0] + pl.program_id(0)) * STEP
    for k in range(2):
        row = where[1] + 8 * k - first

        @pl.when((row >= 0) & (row < STEP))
        def _():
            rows = pl.ds(pl.multiple_of(row, 8), 8)
            acc[rows, :] = acc[rows, :] + window[8 * k : 8 * k + 8, :]

    out[...] = acc[...].astype(out.dtype)


def half_gradient(where, act, cot, err, window, dtype, name):
    tokens = act.shape[0]
    return pl.pallas_call(
        gradient_kernel,
        out_shape=jax.ShapeDtypeStruct((HALF, D), dtype),
        grid_spec=pltpu.PrefetchScalarGridSpec(
            num_scalar_prefetch=1,
            grid=(HALF // STEP,),
            in_specs=[
                pl.BlockSpec((tokens, STEP), lambda i, w: (0, w[0] + i)),
                pl.BlockSpec((tokens, D), lambda i, w: (0, 0)),
                pl.BlockSpec((STEP, D), lambda i, w: (w[0] + i, 0)),
                pl.BlockSpec((16, D), lambda i, w: (0, 0)),
            ],
            out_specs=pl.BlockSpec((STEP, D), lambda i, w: (i, 0)),
            scratch_shapes=[pltpu.VMEM((STEP, D), jnp.float32)],
        ),
        cost_estimate=pl.CostEstimate(
            flops=2 * tokens * HALF * D, bytes_accessed=12 << 20, transcendentals=0
        ),
        name=name,
    )(where, act, cot, err, window)


def pair_kernel(own, got, out):
    for b in range(COLS):
        at = slice(b * BLOCK, (b + 1) * BLOCK)
        both = own[:, at] + got[:, at].astype(jnp.float32)
        out[:, b] = both.astype(jnp.bfloat16).reshape(-1, 8, BLOCK)


def pair_sum(own, got):
    out = pl.pallas_call(
        pair_kernel,
        out_shape=jax.ShapeDtypeStruct((N_CHIPS * PER_CHIP // COLS + 1, COLS, 8, BLOCK), jnp.bfloat16),
        grid=(HALF // STEP,),
        in_specs=[
            pl.BlockSpec((STEP, D), lambda i: (i, 0)),
            pl.BlockSpec((STEP, D), lambda i: (i, 0)),
        ],
        out_specs=pl.BlockSpec((STEP // 8, COLS, 8, BLOCK), lambda i: (i, 0, 0, 0)),
        cost_estimate=pl.CostEstimate(flops=HALF * D, bytes_accessed=7 << 20, transcendentals=0),
        name="pair",
    )(own, got)
    return out


def owner_kernel(parts, out):
    total = jnp.sum(parts[...].astype(jnp.float32), axis=0)
    update = quantized(total).astype(jnp.bfloat16)
    for k in range(N_CHIPS):
        out[k] = update


def owner_update(parts):
    return pl.pallas_call(
        owner_kernel,
        out_shape=jax.ShapeDtypeStruct((N_CHIPS, OWNED, BLOCK), jnp.bfloat16),
        in_specs=[pl.BlockSpec(memory_space=pltpu.VMEM)],
        out_specs=pl.BlockSpec(memory_space=pltpu.VMEM),
        cost_estimate=pl.CostEstimate(
            flops=N_CHIPS * OWNED * BLOCK, bytes_accessed=4 << 20, transcendentals=0
        ),
        name="owner",
    )(parts)


def widen_kernel(where, part, *rest):
    out = rest[-1]
    for b in range(COLS):
        out[:, b * BLOCK : (b + 1) * BLOCK] = (
            part[:, b].astype(jnp.float32).reshape(-1, BLOCK)
        )


def widen(where, part, base, name):
    specs = [pl.BlockSpec((STEP // 8, COLS, 8, BLOCK), lambda i, w: (i, 0, 0, 0))]
    args = [where, part]
    aliases = {}
    if base is not None:
        specs.append(pl.BlockSpec(memory_space=pl.ANY))
        args.append(base)
        aliases = {2: 0}
    return pl.pallas_call(
        widen_kernel,
        out_shape=jax.ShapeDtypeStruct((D, D), jnp.float32),
        grid_spec=pltpu.PrefetchScalarGridSpec(
            num_scalar_prefetch=1,
            grid=(HALF // STEP,),
            in_specs=specs,
            out_specs=pl.BlockSpec((STEP, D), lambda i, w: (w[0] + i, 0)),
        ),
        input_output_aliases=aliases,
        cost_estimate=pl.CostEstimate(flops=HALF * D, bytes_accessed=5 << 20, transcendentals=0),
        name=name,
    )(*args)


def swap_cores(value):
    return lax.ppermute(value, "c", [(0, 1), (1, 0)])


def on_device(activations, cotangent, carried_error, owner_error):
    core = lax.axis_index("c")
    rows = owner_error.shape[0]
    first = lax.axis_index(AXES) * rows
    aligned = first // 8 * 8
    window = lax.dynamic_update_slice(
        jnp.zeros((16, D), jnp.float32), owner_error, (first - aligned, 0)
    )
    steps = HALF // STEP
    mine = jnp.stack([core * steps, aligned]).astype(jnp.int32)
    theirs = jnp.stack([(1 - core) * steps, aligned]).astype(jnp.int32)
    error = carried_error.reshape(D, D)
    to_send = half_gradient(theirs, activations, cotangent, error, window, jnp.bfloat16, "send_half")
    got = swap_cores(to_send)
    own = half_gradient(mine, activations, cotangent, error, window, jnp.float32, "own_half")
    sums = pair_sum(own, got)
    sums = sums.reshape(-1, 8, BLOCK)[: N_CHIPS * PER_CHIP].reshape(N_CHIPS, OWNED, BLOCK)
    parts = lax.all_to_all(sums, CHIPS, 0, 0, tiled=True)
    update = owner_update(parts)
    all_mine = lax.all_to_all(update, CHIPS, 0, 0, tiled=True)
    all_mine = all_mine.reshape(-1, 8, BLOCK)[:TILES].reshape(HALF // 8, COLS, 8, BLOCK)
    all_theirs = swap_cores(all_mine)
    half_out = widen(mine[:1], all_mine, None, "widen_own")
    return widen(theirs[:1], all_theirs, half_out, "widen_other")


def solution(mesh):
    fine = Mesh(mesh.devices.reshape(2, 2, 2, 4, 4), AXES)
    return jax.shard_map(
        on_device,
        mesh=fine,
        in_specs=(P(AXES, None), P(AXES, None), P(AXES, None, None), P(AXES, None)),
        out_specs=P(),
        check_vma=False,
    )
```

time: 501 us -> 116 us (0.23)
  waiting for transfers between devices: 329 us -> 0.01 us
  local copies, waits for them, and re-layouts: 85.1 us -> 5.84 us
  blocking collectives: 10.1 us -> 65.8 us
  Pallas kernels: 0 us -> 37.9 us
  other arithmetic: 27.3 us -> 1.17 us
  starting transfers between devices: 20.5 us -> 4.09 us
  matrix products: 14.4 us -> 0 us
  between operations: 13.5 us -> 0.04 us
    all_gather x1 -> x0, waiting for transfers between devices: 308 us -> none  [side_by_side(): lax.all_gather(both, axis, axis=dim, tiled=True)]
    all_to_all x1 -> x2, blocking collectives: 10.1 us -> 65.8 us  [the longest x1 36.4 us: on_device(): parts = lax.all_to_all(sums, CHIPS, 0, 0, tiled=True)]
    pallas_call x0 -> x6, Pallas kernels: none -> 37.9 us  [the longest x2 21.1 us: half_gradient(): pl.pallas_call(gradient_kernel, out_shape=jax.ShapeDtypeStruct((HALF, D),...]
    mul x4 -> x0, local copies, waits for them, and re-layouts: 27.3 us -> none  [dequantize(): blocks * scales.astype(jnp.float32)[..., None]]
    all_to_all x2 -> x0, waiting for transfers between devices: 20.9 us -> none  [the longest x1 20.9 us: on_device(): lax.all_to_all(levels.reshape(grp_count, dp_count, owner_rows, D), 'dp',...]
    all_to_all x2 -> x0, starting transfers between devices: 20.4 us -> none  [the longest x1 11.4 us: on_device(): lax.all_to_all(scales.reshape(grp_count, dp_count, owner_rows, block_coun...]
    div x3 -> x0, local copies, waits for them, and re-layouts: 19.6 us -> none  [quantize(): blocks / scales.astype(jnp.float32)[..., None]]
    dot_general x1 -> x0, matrix products: 14.4 us -> none  [on_device(): lax.dot_general(activations, cotangent, (((0,), (0,)), ((), ())), preferr...]
  transfers between devices with their start and end apart: 3 -> 2, of which waited for: 2 -> 0; matrix products, arithmetic and copies ran while one was open for 13% -> 1% of each run, Pallas kernels for 0% -> 13%
where the time goes in v1:
time: 116 us; the launch traced here: 115 us
  blocking collectives  65.8 us (57%)
  Pallas kernels  37.9 us (33%)
  local copies, waits for them, and re-layouts  5.84 us (5%)
  starting transfers between devices  4.09 us (4%)
  other arithmetic  1.17 us (1%)
    all_to_all x1, blocking collectives, on_device(): parts = lax.all_to_all(sums, CHIPS, 0, 0, tiled=True)  36.4 us
    all_to_all x1, blocking collectives, on_device(): all_mine = lax.all_to_all(update, CHIPS, 0, 0, tiled=True)  29.4 us
    pallas_call x2, Pallas kernels, half_gradient(): pl.pallas_call(gradient_kernel, out_shape=jax.ShapeDtypeStruct((HALF, D),...  21.1 us
    pallas_call x2, Pallas kernels, widen(): pl.pallas_call(widen_kernel, out_shape=jax.ShapeDtypeStruct((D, D), jnp.f...  8.84 us
    pallas_call x1, Pallas kernels, pair_sum(): pl.pallas_call(pair_kernel, out_shape=jax.ShapeDtypeStruct((N_CHIPS * PER...  4.95 us
    ppermute x2, starting transfers between devices, swap_cores(): return lax.ppermute(value, 'c', [(0, 1), (1, 0)])  4.09 us
    pallas_call x1, Pallas kernels, owner_update(): pl.pallas_call(owner_kernel, out_shape=jax.ShapeDtypeStruct((N_CHIPS, OWN...  3.01 us
    unnamed x8, local copies, waits for them, and re-layouts  2.95 us
  transfers between devices with their start and end apart: 2, of which 0 were waited for; matrix products, arithmetic and copies ran while one was open for 1% of the time, Pallas kernels for 13%

profile of v1, /device:TPU:1, one launch (start us, length us, event | category | flops | bytes accessed | tf_op | source)
XLA Modules:
  0.0 114.8 jit_solution(3845963632151036546)
XLA Ops:
  0.0 0.6 pad_add_fusion.1.where
  0.6 1.2 %dynamic_update_slice.3.window = f32[16,1280]{1,0:T(8,128)S(1)} dynamic-update-slice(f32[16,1280]{1,0:T(8,128)S(1)} %broadcast_in_dim.3, f32[10,1280]{1,0:T(8,128)} %param.7, s32[]{:T(128)S(6)} %select_n.9, s32[]{:T(128)} %constant.48.clone.1) | dynamic-update-slice | bytes 102404 | tf_op jit(solution)/shard_map/dynamic_update_slice | solution.py:157
  1.8 0.0 copy-start.3
  1.8 0.6 copy-done.3
  2.5 10.3 %send_half.1 = bf16[640,1280]{1,0:T(8,128)(2,1)} custom-call(s32[2]{0:T(128)} %pad_add_fusion.1.where, bf16[2048,1280]{1,0:T(8,128)(2,1)} %act.3, bf16[2048,1280]{1,0:T(8,128)(2,1)} %cot.3, f32[1280,1280]{1,0:T(8,128)} %bitcast.8, f32[16,1280]{1,0:T(8,128)} %copy-done.3), custom_call_target="tpu_custom_call" | custom-call | flops 3355443200 | bytes 12582912 | tf_op jit(solution)/shard_map/send_half/pallas_call | solution.py:52
  12.8 1.4 %collective-permute-start = (bf16[640,1280]{1,0:T(8,128)(2,1)}, bf16[640,1280]{1,0:T(8,128)(2,1)S(1)}, u32[]{:S(2)}, u32[]{:S(2)}) collective-permute-start(bf16[640,1280]{1,0:T(8,128)(2,1)} %send_half.1), channel_id=1, source_target_pairs={{0,32},{32,0},{1,33},{33,1},{2,34},{34,2},{3,35},{35,3},{4,36},{36... | collective-permute-start | bytes 4915208 | tf_op jit(solution)/shard_map/ppermute | solution.py:149
  14.2 0.6 pad_add_fusion.where
  14.8 10.7 %own_half.1.own = f32[640,1280]{1,0:T(8,128)} custom-call(s32[2]{0:T(128)} %pad_add_fusion.where, bf16[2048,1280]{1,0:T(8,128)(2,1)} %act.3, bf16[2048,1280]{1,0:T(8,128)(2,1)} %cot.3, f32[1280,1280]{1,0:T(8,128)} %bitcast.9, f32[16,1280]{1,0:T(8,128)} %copy-done.3), custom_call_target="tpu_custom_call" | custom-call | flops 3355443200 | bytes 12582912 | tf_op jit(solution)/shard_map/own_half/pallas_call | solution.py:52
  25.5 0.0 collective-permute-done.got
  25.5 0.0 copy-start.1
  25.5 1.2 %copy-done.1 = bf16[640,1280]{1,0:T(8,128)(2,1)} copy-done((bf16[640,1280]{1,0:T(8,128)(2,1)}, bf16[640,1280]{1,0:T(8,128)(2,1)S(1)}, u32[]{:S(2)}) %copy-start.1) | copy-done | bytes 1638424
  26.6 4.9 %pair.1 = bf16[84,10,8,128]{3,2,1,0:T(8,128)(2,1)} custom-call(f32[640,1280]{1,0:T(8,128)} %own_half.1.own, bf16[640,1280]{1,0:T(8,128)(2,1)} %copy-done.1), custom_call_target="tpu_custom_call" | custom-call | flops 819200 | bytes 7340032 | tf_op jit(solution)/shard_map/pair/pallas_call | solution.py:82
  31.6 1.6 %slice.8 = bf16[832,8,128]{2,1,0:T(8,128)(2,1)S(1)} slice(bf16[840,8,128]{2,1,0:T(8,128)(2,1)} %bitcast.10), slice={[0:832], [0:8], [0:128]} | slice | bytes 3407872 | tf_op jit(solution)/shard_map/slice | solution.py:168
  33.2 36.4 %all_to_all.10.parts = bf16[64,104,128]{2,1,0:T(8,128)(2,1)} all-to-all(bf16[64,104,128]{2,1,0:T(8,128)(2,1)S(1)} %bitcast.11), channel_id=1, replica_groups=mesh['zl'=2,'c'=2,'zh'=2,'y'=4,'x'=4] {'zl','zh','y','x'}, dimensions={0} | all-to-all | bytes 3407872 | tf_op jit(solution)/shard_map/all_to_all | solution.py:169
  69.5 3.0 %owner.1 = bf16[64,104,128]{2,1,0:T(8,128)(2,1)} custom-call(bf16[64,104,128]{2,1,0:T(8,128)(2,1)} %all_to_all.10.parts), custom_call_target="tpu_custom_call" | custom-call | flops 851968 | bytes 4194304 | tf_op jit(solution)/shard_map/owner/pallas_call | solution.py:105
  72.5 29.4 %all_to_all.11 = bf16[64,104,128]{2,1,0:T(8,128)(2,1)S(1)} all-to-all(bf16[64,104,128]{2,1,0:T(8,128)(2,1)} %owner.1), channel_id=1, replica_groups=mesh['zl'=2,'c'=2,'zh'=2,'y'=4,'x'=4] {'zl','zh','y','x'}, dimensions={0} | all-to-all | bytes 3407872 | tf_op jit(solution)/shard_map/all_to_all | solution.py:171
  101.9 0.1 slice.9
  102.0 0.0 copy-start
  102.0 2.7 %collective-permute-start.1 = (bf16[80,10,8,128]{3,2,1,0:T(8,128)(2,1)S(1)}, bf16[80,10,8,128]{3,2,1,0:T(8,128)(2,1)S(1)}, u32[]{:S(2)}, u32[]{:S(2)}) collective-permute-start(bf16[80,10,8,128]{3,2,1,0:T(8,128)(2,1)S(1)} %bitcast.13), channel_id=1, source_target_pairs={{0,32},{32,0},{1,33},{33,1},{2,34},{34,2},{3,35},{35,3},{4,36},{36... | collective-permute-start | bytes 4915208 | tf_op jit(solution)/shard_map/ppermute | solution.py:149
  104.8 0.0 copy-done
  104.8 4.4 %widen_own.1.rest_0_ = f32[1280,1280]{1,0:T(8,128)} custom-call(s32[1]{0:T(128)} %bitcast.1.where, bf16[80,10,8,128]{3,2,1,0:T(8,128)(2,1)} %bitcast.14), custom_call_target="tpu_custom_call" | custom-call | flops 819200 | bytes 5242880 | tf_op jit(solution)/shard_map/widen_own/pallas_call | solution.py:133
  109.2 0.0 collective-permute-done.1.part
  109.2 0.0 copy-start.2
  109.2 1.2 %copy-done.2 = bf16[80,10,8,128]{3,2,1,0:T(8,128)(2,1)} copy-done((bf16[80,10,8,128]{3,2,1,0:T(8,128)(2,1)}, bf16[80,10,8,128]{3,2,1,0:T(8,128)(2,1)S(1)}, u32[]{:S(2)}) %copy-start.2) | copy-done | bytes 1638424
  110.4 4.4 %widen_other.1 = f32[1280,1280]{1,0:T(8,128)} custom-call(s32[1]{0:T(128)} %bitcast.where, bf16[80,10,8,128]{3,2,1,0:T(8,128)(2,1)} %copy-done.2, f32[1280,1280]{1,0:T(8,128)} %widen_own.1.rest_0_), custom_call_target="tpu_custom_call", output_to_operand_aliasing={{}: (2, {})} | custom-call | flops 819200 | bytes 5242880 | tf_op jit(solution)/shard_map/widen_other/pallas_call | solution.py:133
  (1 shorter events, 0.0 us)
Async XLA Ops:
  1.8 0.6 copy-start.3
  12.8 12.7 %collective-permute-start = (bf16[640,1280]{1,0:T(8,128)(2,1)}, bf16[640,1280]{1,0:T(8,128)(2,1)S(1)}, u32[]{:S(2)}, u32[]{:S(2)}) collective-permute-start(bf16[640,1280]{1,0:T(8,128)(2,1)} %send_half.1), channel_id=1, source_target_pairs={{0,32},{32,0},{1,33},{33,1},{2,34},{34,2},{3,35},{35,3},{4,36},{36... | collective-permute-start | bytes 4915208 | tf_op jit(solution)/shard_map/ppermute | solution.py:149
  25.5 1.2 %copy-start.1 = (bf16[640,1280]{1,0:T(8,128)(2,1)}, bf16[640,1280]{1,0:T(8,128)(2,1)S(1)}, u32[]{:S(2)}) copy-start(bf16[640,1280]{1,0:T(8,128)(2,1)S(1)} %collective-permute-done.got) | copy-start | bytes 4915204
  102.0 2.7 %copy-start = (bf16[800,8,128]{2,1,0:T(8,128)(2,1)}, bf16[800,8,128]{2,1,0:T(8,128)(2,1)S(1)}, u32[]{:S(2)}) copy-start(bf16[800,8,128]{2,1,0:T(8,128)(2,1)S(1)} %slice.9) | copy-start | bytes 4915204
  102.0 7.1 %collective-permute-start.1 = (bf16[80,10,8,128]{3,2,1,0:T(8,128)(2,1)S(1)}, bf16[80,10,8,128]{3,2,1,0:T(8,128)(2,1)S(1)}, u32[]{:S(2)}, u32[]{:S(2)}) collective-permute-start(bf16[80,10,8,128]{3,2,1,0:T(8,128)(2,1)S(1)} %bitcast.13), channel_id=1, source_target_pairs={{0,32},{32,0},{1,33},{33,1},{2,34},{34,2},{3,35},{35,3},{4,36},{36... | collective-permute-start | bytes 4915208 | tf_op jit(solution)/shard_map/ppermute | solution.py:149
  109.2 1.2 %copy-start.2 = (bf16[80,10,8,128]{3,2,1,0:T(8,128)(2,1)}, bf16[80,10,8,128]{3,2,1,0:T(8,128)(2,1)S(1)}, u32[]{:S(2)}) copy-start(bf16[80,10,8,128]{3,2,1,0:T(8,128)(2,1)S(1)} %collective-permute-done.1.part) | copy-start | bytes 4915204

commit v2 on v1

v2 whole, which is shorter than its diff:
```python
import jax
import jax.numpy as jnp
import numpy as np
from jax import lax
from jax.experimental import pallas as pl
from jax.experimental.pallas import tpu as pltpu
from jax.sharding import Mesh
from jax.sharding import PartitionSpec as P


D = 1280
BLOCK = 128
HALF = D // 2
COLS = D // BLOCK
AXES = ("zl", "c", "zh", "y", "x")
SIZES = (2, 2, 2, 4, 4)
QUARTER = HALF // 4
TILES = QUARTER // 8 * COLS
PER_CHIP = -(-TILES // 16)
OWNED = PER_CHIP * 8
CHUNK = 512
ORDER = (2, 1, 3, 0)
MIB = 1 << 20
GRANT = 46


def device(zl, c, zh, y, x):
    return int(np.ravel_multi_index((zl, c, zh, y, x), SIZES))


def line(core, lead):
    spots = [(zl, zh, o) for zl in range(2) for zh in range(2) for o in range(4)]
    if core == 0:
        return [device(zl, 0, zh, o, lead) for zl, zh, o in spots]
    return [device(zl, 1, zh, lead, o) for zl, zh, o in spots]


SIXTEENS = [line(core, lead) for core in range(2) for lead in range(4)]


def from_ahead(k):
    pairs = []
    for core in range(2):
        for lead in range(4):
            pairs += list(zip(line(core, (lead + k) % 4), line(core, lead)))
    return pairs


def to_ahead(k):
    return [(source, target) for target, source in from_ahead(k)]


def params(mib, **more):
    return pltpu.CompilerParams(vmem_limit_bytes=mib * MIB, **more)


def quantized(v):
    largest = jnp.max(jnp.abs(v), axis=-1, keepdims=True)
    scale = ((largest + 1e-06) / 127.0).astype(jnp.bfloat16).astype(jnp.float32)
    level = (v * (1.0 / scale)).astype(jnp.bfloat16).astype(jnp.float32)
    return level * scale


def multiplied(a, c):
    return lax.dot_general(a, c, (((0,), (0,)), ((), ())), preferred_element_type=jnp.float32)


def gradient_kernel(places, spot, act, cot, error, owner, sent, kept, acc, err, sem):
    load = pltpu.make_async_copy(error, err, sem)

    def step(a, c):
        first = pl.program_id(0) == 0

        @pl.when(first)
        def _():
            load.start()
            for m in range(0, D, 256):
                acc[m : m + 256, :] = multiplied(a[:, m : m + 256], c[...])

        @pl.when(jnp.logical_not(first))
        def _():
            for m in range(0, D, 256):
                acc[m : m + 256, :] = acc[m : m + 256, :] + multiplied(a[:, m : m + 256], c[...])

    pltpu.emit_pipeline(
        step,
        grid=(act.shape[0] // CHUNK,),
        in_specs=[
            pl.BlockSpec((CHUNK, D), lambda i: (i, 0)),
            pl.BlockSpec((CHUNK, D), lambda i: (i, 0)),
        ],
    )(act, cot)
    load.wait()
    row = spot[0]
    aligned = row // 8 * 8
    for half, out in enumerate((sent, kept)):

        @pl.loop(0, 4)
        def _(k):
            start = pl.multiple_of(places[half] + (places[2 + half] + k) % 4 * QUARTER, 32)
            rows = pl.ds(start, QUARTER)
            for b in range(COLS):
                at = slice(b * BLOCK, (b + 1) * BLOCK)
                block = quantized(acc[rows, at] + err[rows, at])
                acc[rows, at] = block
                out[k, :, at] = block.astype(out.dtype)

        @pl.loop(0, 2)
        def _(i):
            tile = aligned + 8 * i
            inside = tile - places[half]

            @pl.when((inside >= 0) & (inside < HALF))
            def _():
                k = (inside // QUARTER + 4 - places[2 + half]) % 4
                add_owner(acc, owner, out, tile, row, k, inside % QUARTER)


def add_owner(acc, owner, out, tile, row, k, at):
    for shift in (-8, -6, -4, -2, 0, 2, 4, 6):

        @pl.when(row - tile == shift)
        def _():
            low, high = max(shift, 0), min(shift + 10, 8)
            mine = owner[low - shift : high - shift, :]
            mine = jnp.pad(mine, ((low, 8 - high), (0, 0)))
            total = acc[pl.ds(pl.multiple_of(tile, 8), 8), :] + mine
            out[k, pl.ds(pl.multiple_of(at, 8), 8), :] = total.astype(out.dtype)


def gradient(places, spot, act, cot, error, owner):
    return pl.pallas_call(
        gradient_kernel,
        out_shape=(
            jax.ShapeDtypeStruct((4, QUARTER, D), jnp.bfloat16),
            jax.ShapeDtypeStruct((4, QUARTER, D), jnp.float32),
        ),
        in_specs=[pl.BlockSpec(memory_space=pltpu.SMEM)] * 2
        + [pl.BlockSpec(memory_space=pltpu.HBM)] * 3
        + [pl.BlockSpec(memory_space=pltpu.VMEM)],
        out_specs=(pl.BlockSpec(memory_space=pltpu.VMEM),) * 2,
        scratch_shapes=[
            pltpu.VMEM((D, D), jnp.float32),
            pltpu.VMEM((D, D), jnp.float32),
            pltpu.SemaphoreType.DMA,
        ],
        compiler_params=params(GRANT),
        cost_estimate=pl.CostEstimate(
            flops=2 * act.shape[0] * D * D, bytes_accessed=17 * MIB, transcendentals=0
        ),
        name="gradient",
    )(places, spot, act, cot, error, owner)


def pair_kernel(kept, got, out):
    out[...] = (kept[0] + got[...].astype(jnp.float32)).astype(out.dtype)


def pair(kept, got, k, dtype):
    return pl.pallas_call(
        pair_kernel,
        out_shape=jax.ShapeDtypeStruct((QUARTER, D), dtype),
        grid=(1,),
        in_specs=[
            pl.BlockSpec((1, QUARTER, D), lambda i: (k, 0, 0)),
            pl.BlockSpec((QUARTER, D), lambda i: (0, 0)),
        ],
        out_specs=pl.BlockSpec((QUARTER, D), lambda i: (0, 0)),
        compiler_params=params(6),
        cost_estimate=pl.CostEstimate(flops=1 << 28, bytes_accessed=2 * MIB, transcendentals=0),
    )(kept, got)


def total_kernel(own, *rest):
    out = rest[-1]
    for b in range(COLS):
        at = slice(b * BLOCK, (b + 1) * BLOCK)
        total = own[:, at]
        for got in rest[:-1]:
            total = total + got[:, at].astype(jnp.float32)
        total = total.astype(jnp.bfloat16).reshape(QUARTER // 8, 8, BLOCK)
        for r in range(QUARTER // 8):
            out[r * COLS + b] = total[r]
    out[TILES:] = jnp.zeros_like(out[TILES:])


def total_of(own, others):
    return pl.pallas_call(
        total_kernel,
        out_shape=jax.ShapeDtypeStruct((16 * PER_CHIP, 8, BLOCK), jnp.bfloat16),
        in_specs=[pl.BlockSpec(memory_space=pltpu.VMEM)] * (1 + len(others)),
        out_specs=pl.BlockSpec(memory_space=pltpu.VMEM),
        compiler_params=params(4),
        cost_estimate=pl.CostEstimate(flops=4 * QUARTER * D, bytes_accessed=2 * MIB, transcendentals=0),
        name="total",
    )(own, *others)


def owner_kernel(parts, out):
    total = parts[0].astype(jnp.float32)
    for k in range(1, parts.shape[0]):
        total = total + parts[k].astype(jnp.float32)
    update = quantized(total).astype(jnp.bfloat16)
    for k in range(out.shape[0]):
        out[k] = update


def owner_update(parts):
    return pl.pallas_call(
        owner_kernel,
        out_shape=jax.ShapeDtypeStruct((16, OWNED, BLOCK), jnp.bfloat16),
        in_specs=[pl.BlockSpec(memory_space=pltpu.VMEM)],
        out_specs=pl.BlockSpec(memory_space=pltpu.VMEM),
        compiler_params=params(8),
        cost_estimate=pl.CostEstimate(
            flops=parts.size, bytes_accessed=2 * MIB, transcendentals=0
        ),
        name="owner",
    )(parts)


def widen_kernel(where, part, *rest):
    out = rest[-1]
    for r in range(QUARTER // 8):
        for b in range(COLS):
            out[r * 8 : r * 8 + 8, b * BLOCK : (b + 1) * BLOCK] = part[r * COLS + b].astype(
                jnp.float32
            )


def widen(where, part, base):
    specs = [pl.BlockSpec((TILES, 8, BLOCK), lambda i, w: (0, 0, 0))]
    args = [where, part]
    aliases = {}
    if base is not None:
        specs.append(pl.BlockSpec(memory_space=pl.ANY))
        args.append(base)
        aliases = {2: 0}
    return pl.pallas_call(
        widen_kernel,
        out_shape=jax.ShapeDtypeStruct((D, D), jnp.float32),
        grid_spec=pltpu.PrefetchScalarGridSpec(
            num_scalar_prefetch=1,
            grid=(1,),
            in_specs=specs,
            out_specs=pl.BlockSpec((QUARTER, D), lambda i, w: (w[0], 0)),
        ),
        input_output_aliases=aliases,
        compiler_params=params(4),
        cost_estimate=pl.CostEstimate(
            flops=1 << 30, bytes_accessed=MIB, transcendentals=0
        ),
        name="widen",
    )(*args)


def swap_cores(value):
    return lax.ppermute(value, "c", [(0, 1), (1, 0)])


def one(value):
    return value.astype(jnp.int32).reshape(1)


def on_device(activations, cotangent, carried_error, owner_error):
    core = lax.axis_index("c")
    x, y = lax.axis_index("x"), lax.axis_index("y")
    lead = jnp.where(core == 0, x, y)
    other_lead = x + y - lead
    spot = one(lax.axis_index(AXES) * owner_error.shape[0])
    error = carried_error.reshape(D, D)
    places = jnp.stack([(1 - core) * HALF, core * HALF, other_lead, lead]).astype(jnp.int32)
    sent, kept = gradient(places, spot, activations, cotangent, error, owner_error)
    got = {}
    for k in ORDER:
        got[k] = swap_cores(sent[k])
    arrived = []
    for k in ORDER:
        whole = k == 0
        piece = pair(kept, got[k], k, jnp.float32 if whole else jnp.bfloat16)
        if whole:
            own = piece
        else:
            arrived.append(lax.ppermute(piece, AXES, to_ahead(k)))
    parts = total_of(own, arrived).reshape(16, OWNED, BLOCK)
    parts = lax.all_to_all(parts, AXES, 0, 0, axis_index_groups=SIXTEENS, tiled=True)
    update = owner_update(parts)
    mine = lax.all_to_all(update, AXES, 0, 0, axis_index_groups=SIXTEENS, tiled=True)
    mine = mine.reshape(16 * PER_CHIP, 8, BLOCK)[:TILES]
    pieces = [(0, mine)]
    for k in (2, 1, 3):
        pieces.append((k, lax.ppermute(mine, AXES, from_ahead(k))))
    out = None
    for k, piece in pieces:
        if out is not None:
            piece, out = lax.optimization_barrier((piece, out))
        other = swap_cores(piece)
        out = widen(one(core * 4 + (lead + k) % 4), piece, out)
        out = widen(one((1 - core) * 4 + (other_lead + k) % 4), other, out)
    return out


def solution(mesh):
    fine = Mesh(mesh.devices.reshape(SIZES), AXES)
    return jax.shard_map(
        on_device,
        mesh=fine,
        in_specs=(P(AXES, None), P(AXES, None), P(AXES, None, None), P(AXES, None)),
        out_specs=P(),
        check_vma=False,
    )
```

time: 116 us -> 93.5 us (0.81)
  blocking collectives: 65.8 us -> 28.1 us
  waiting for transfers between devices: 0.01 us -> 28.6 us
  Pallas kernels: 37.9 us -> 21.4 us
  starting transfers between devices: 4.09 us -> 14 us
  local copies, waits for them, and re-layouts: 5.84 us -> 1.02 us
    all_to_all x2, blocking collectives: 65.8 us -> 28.1 us  [the longest x1 16 us: on_device(): lax.all_to_all(parts, AXES, 0, 0, axis_index_groups=SIXTEENS, tiled=True)]
    ppermute x0 -> x6, waiting for transfers between devices: none -> 27.2 us  [the longest x3 16.5 us: on_device(): pieces.append((k, lax.ppermute(mine, AXES, from_ahead(k))))]
    pallas_call x4 -> x7, Pallas kernels: 29 us -> 13.9 us  [the longest x1 13.1 us: gradient(): pl.pallas_call(gradient_kernel, out_shape=(jax.ShapeDtypeStruct((4, QUART...]
    ppermute x0 -> x6, starting transfers between devices: none -> 6.4 us  [the longest x3 4.69 us: on_device(): arrived.append(lax.ppermute(piece, AXES, to_ahead(k)))]
    ppermute x2 -> x8, starting transfers between devices: 4.09 us -> 7.56 us  [swap_cores(): return lax.ppermute(value, 'c', [(0, 1), (1, 0)])]
    unnamed x8 -> x2, local copies, waits for them, and re-layouts: 2.95 us -> 0.89 us
    slice x2 -> x1, local copies, waits for them, and re-layouts: 1.67 us -> 0.03 us  [on_device(): mine = mine.reshape(16 * PER_CHIP, 8, BLOCK)[:TILES]]
    ppermute x2 -> x8, waiting for transfers between devices: 0.01 us -> 1.35 us  [swap_cores(): return lax.ppermute(value, 'c', [(0, 1), (1, 0)])]
  transfers between devices with their start and end apart: 2 -> 14, of which waited for: 0 -> 8; matrix products, arithmetic and copies ran while one was open for 1% -> 0% of each run, Pallas kernels for 13% -> 7%
where the time goes in v2:
time: 93.5 us; the launch traced here: 93.3 us
  waiting for transfers between devices  28.6 us (31%)
  blocking collectives  28.1 us (30%)
  Pallas kernels  21.4 us (23%)
  starting transfers between devices  14 us (15%)
  local copies, waits for them, and re-layouts  1.02 us (1%)
    ppermute x3, waiting for transfers between devices, on_device(): pieces.append((k, lax.ppermute(mine, AXES, from_ahead(k))))  16.5 us
    all_to_all x1, blocking collectives, on_device(): lax.all_to_all(parts, AXES, 0, 0, axis_index_groups=SIXTEENS, tiled=True)  16 us
    pallas_call x1, Pallas kernels, gradient(): pl.pallas_call(gradient_kernel, out_shape=(jax.ShapeDtypeStruct((4, QUART...  13.1 us
    all_to_all x1, blocking collectives, on_device(): lax.all_to_all(update, AXES, 0, 0, axis_index_groups=SIXTEENS, tiled=True)  12.1 us
    ppermute x3, waiting for transfers between devices, on_device(): arrived.append(lax.ppermute(piece, AXES, to_ahead(k)))  10.8 us
    ppermute x8, starting transfers between devices, swap_cores(): return lax.ppermute(value, 'c', [(0, 1), (1, 0)])  7.56 us
    pallas_call x8, Pallas kernels, widen(): pl.pallas_call(widen_kernel, out_shape=jax.ShapeDtypeStruct((D, D), jnp.f...  7.56 us
    ppermute x3, starting transfers between devices, on_device(): arrived.append(lax.ppermute(piece, AXES, to_ahead(k)))  4.69 us
  transfers between devices with their start and end apart: 14, of which 8 were waited for; matrix products, arithmetic and copies ran while one was open for 0% of the time, Pallas kernels for 7%

profile of v2, /device:TPU:1, one launch (start us, length us, event | category | flops | bytes accessed | tf_op | source)
XLA Modules:
  0.0 93.3 jit_solution(721017592341704337)
XLA Ops:
  0.0 0.1 pad_add_fusion.places
  0.1 0.0 copy-start
  0.1 0.9 copy-done
  1.0 13.1 %gradient.1 = (bf16[4,160,1280]{2,1,0:T(8,128)(2,1)S(1)}, f32[4,160,1280]{2,1,0:T(8,128)S(1)}) custom-call(s32[4]{0:T(128)S(1)} %pad_add_fusion.places, s32[1]{0:T(128)} %bitcast.5.spot, bf16[2048,1280]{1,0:T(8,128)(2,1)} %act.1, bf16[2048,1280]{1,0:T(8,128)(2,1)} %cot.1, f32[1280,1280]{1,0:T(8,128)} %bitcast.26, f32[10,1280]{1,0:T(8,128)S(1)} %copy-done), custom_call_target="tpu_custom_call" | custom-call | flops 6710886400 | bytes 17825792 | tf_op jit(solution)/shard_map/gradient/pallas_call | solution.py:132
  14.1 0.1 slice_bitcast_fusion
  14.2 1.5 %collective-permute-start.5 = (bf16[160,1280]{1,0:T(8,128)(2,1)S(1)}, bf16[160,1280]{1,0:T(8,128)(2,1)S(1)}, u32[]{:S(2)}, u32[]{:S(2)}) collective-permute-start(bf16[160,1280]{1,0:T(8,128)(2,1)S(1)} %get-tuple-element.21), channel_id=1, source_target_pairs={{0,32},{32,0},{1,33},{33,1},{2,34},{34,2},{3,35},{35,3},{4,36},{36... | collective-permute-start | bytes 1228808 | tf_op jit(solution)/shard_map/ppermute | solution.py:258
  15.7 0.1 collective-permute-start.3
  15.8 0.4 collective-permute-start.1
  16.2 0.1 collective-permute-start
  16.3 0.8 collective-permute-done.5.got
  17.1 0.1 shard_map.49
  17.2 2.9 %collective-permute-start.6 = (bf16[160,1280]{1,0:T(8,128)(2,1)S(1)}, bf16[160,1280]{1,0:T(8,128)(2,1)S(1)}, u32[]{:S(2)}, u32[]{:S(2)}) collective-permute-start(bf16[160,1280]{1,0:T(8,128)(2,1)S(1)} %shard_map.49), channel_id=1, source_target_pairs={{0,3},{4,7},{8,11},{12,15},{16,19},{20,23},{24,27},{28,31},{64,67}... | collective-permute-start | bytes 1228808 | tf_op jit(solution)/shard_map/ppermute | solution.py:284
  20.1 0.0 collective-permute-done.3.got
  20.1 0.1 shard_map.48
  20.2 0.1 collective-permute-start.4
  20.3 0.0 collective-permute-done.1.got
  20.3 0.1 shard_map.47
  20.4 1.7 %collective-permute-start.2 = (bf16[160,1280]{1,0:T(8,128)(2,1)S(1)}, bf16[160,1280]{1,0:T(8,128)(2,1)S(1)}, u32[]{:S(2)}, u32[]{:S(2)}) collective-permute-start(bf16[160,1280]{1,0:T(8,128)(2,1)S(1)} %shard_map.47), channel_id=1, source_target_pairs={{0,2},{4,6},{8,10},{12,14},{16,18},{20,22},{24,26},{28,30},{64,66}... | collective-permute-start | bytes 1228808 | tf_op jit(solution)/shard_map/ppermute | solution.py:284
  22.1 0.0 collective-permute-done.got
  22.1 0.1 shard_map.46.own
  22.2 7.2 %collective-permute-done.6.rest_2_ = bf16[160,1280]{1,0:T(8,128)(2,1)S(1)} collective-permute-done((bf16[160,1280]{1,0:T(8,128)(2,1)S(1)}, bf16[160,1280]{1,0:T(8,128)(2,1)S(1)}, u32[]{:S(2)}, u32[]{:S(2)}) %collective-permute-start.6) | collective-permute-done | bytes 409632 | tf_op jit(solution)/shard_map/ppermute | solution.py:284
  29.4 3.6 %collective-permute-done.4.rest_1_ = bf16[160,1280]{1,0:T(8,128)(2,1)S(1)} collective-permute-done((bf16[160,1280]{1,0:T(8,128)(2,1)S(1)}, bf16[160,1280]{1,0:T(8,128)(2,1)S(1)}, u32[]{:S(2)}, u32[]{:S(2)}) %collective-permute-start.4) | collective-permute-done | bytes 409632 | tf_op jit(solution)/shard_map/ppermute | solution.py:284
  32.9 0.0 collective-permute-done.2.rest_0_
  32.9 0.2 total.1
  33.1 16.0 %all_to_all.10.parts = bf16[16,104,128]{2,1,0:T(8,128)(2,1)S(1)} all-to-all(bf16[16,104,128]{2,1,0:T(8,128)(2,1)S(1)} %bitcast.24), channel_id=1, replica_groups={{0,4,8,12,16,20,24,28,64,68,72,76,80,84,88,92},{1,5,9,13,17,21,25,29,65..., dimensions={0} | all-to-all | bytes 851968 | tf_op jit(solution)/shard_map/all_to_all | solution.py:286
  49.2 0.2 owner.3
  49.3 12.1 %all_to_all.11 = bf16[16,104,128]{2,1,0:T(8,128)(2,1)S(1)} all-to-all(bf16[16,104,128]{2,1,0:T(8,128)(2,1)S(1)} %owner.3), channel_id=1, replica_groups={{0,4,8,12,16,20,24,28,64,68,72,76,80,84,88,92},{1,5,9,13,17,21,25,29,65..., dimensions={0} | all-to-all | bytes 851968 | tf_op jit(solution)/shard_map/all_to_all | solution.py:288
  61.5 2.8 %collective-permute-start.10 = (bf16[200,8,128]{2,1,0:T(8,128)(2,1)S(1)}, bf16[200,8,128]{2,1,0:T(8,128)(2,1)S(1)}, u32[]{:S(2)}, u32[]{:S(2)}) collective-permute-start(bf16[200,8,128]{2,1,0:T(8,128)(2,1)S(1)} %slice.20.part), channel_id=1, source_target_pairs={{0,32},{32,0},{1,33},{33,1},{2,34},{34,2},{3,35},{35,3},{4,36},{36... | collective-permute-start | bytes 1228808 | tf_op jit(solution)/shard_map/ppermute | solution.py:258
  64.3 0.9 collective-permute-start.9
  65.1 0.9 %widen.8.rest_0_ = f32[1280,1280]{1,0:T(8,128)} custom-call(s32[1]{0:T(128)} %bitcast.16.where, bf16[200,8,128]{2,1,0:T(8,128)(2,1)S(1)} %slice.20.part), custom_call_target="tpu_custom_call" | custom-call | flops 1073741824 | bytes 1048576 | tf_op jit(solution)/shard_map/widen/pallas_call | solution.py:239
  66.1 0.0 collective-permute-done.10.part
  66.1 0.9 %widen.9.rest_0_ = f32[1280,1280]{1,0:T(8,128)} custom-call(s32[1]{0:T(128)} %bitcast.15.where, bf16[200,8,128]{2,1,0:T(8,128)(2,1)S(1)} %collective-permute-done.10.part, f32[1280,1280]{1,0:T(8,128)} %widen.8.rest_0_), custom_call_target="tpu_custom_call", output_to_operand_aliasing={{}: (2, {})} | custom-call | flops 1073741824 | bytes 1048576 | tf_op jit(solution)/shard_map/widen/pallas_call | solution.py:239
  67.0 5.8 %collective-permute-done.9.part = bf16[200,8,128]{2,1,0:T(8,128)(2,1)S(1)} collective-permute-done((bf16[200,8,128]{2,1,0:T(8,128)(2,1)S(1)}, bf16[200,8,128]{2,1,0:T(8,128)(2,1)S(1)}, u32[]{:S(2)}, u32[]{:S(2)}) %collective-permute-start.9) | collective-permute-done | bytes 409632 | tf_op jit(solution)/shard_map/ppermute | solution.py:292
  72.9 0.9 %collective-permute-start.11 = (bf16[200,8,128]{2,1,0:T(8,128)(2,1)S(1)}, bf16[200,8,128]{2,1,0:T(8,128)(2,1)S(1)}, u32[]{:S(2)}, u32[]{:S(2)}) collective-permute-start(bf16[200,8,128]{2,1,0:T(8,128)(2,1)S(1)} %collective-permute-done.9.part), channel_id=1, source_target_pairs={{0,32},{32,0},{1,33},{33,1},{2,34},{34,2},{3,35},{35,3},{4,36},{36... | collective-permute-start | bytes 1228808 | tf_op jit(solution)/shard_map/ppermute | solution.py:258
  73.8 0.6 collective-permute-start.8
  74.4 0.9 %widen.10.rest_0_ = f32[1280,1280]{1,0:T(8,128)} custom-call(s32[1]{0:T(128)} %bitcast.17.where, bf16[200,8,128]{2,1,0:T(8,128)(2,1)S(1)} %collective-permute-done.9.part, f32[1280,1280]{1,0:T(8,128)} %widen.9.rest_0_), custom_call_target="tpu_custom_call", output_to_operand_aliasing={{}: (2, {})} | custom-call | flops 1073741824 | bytes 1048576 | tf_op jit(solution)/shard_map/widen/pallas_call | solution.py:239
  75.4 0.0 collective-permute-done.11.part
  75.4 0.9 %widen.11.rest_0_ = f32[1280,1280]{1,0:T(8,128)} custom-call(s32[1]{0:T(128)} %bitcast.14.where, bf16[200,8,128]{2,1,0:T(8,128)(2,1)S(1)} %collective-permute-done.11.part, f32[1280,1280]{1,0:T(8,128)} %widen.10.rest_0_), custom_call_target="tpu_custom_call", output_to_operand_aliasing={{}: (2, {})} | custom-call | flops 1073741824 | bytes 1048576 | tf_op jit(solution)/shard_map/widen/pallas_call | solution.py:239
  76.3 4.6 %collective-permute-done.8.part = bf16[200,8,128]{2,1,0:T(8,128)(2,1)S(1)} collective-permute-done((bf16[200,8,128]{2,1,0:T(8,128)(2,1)S(1)}, bf16[200,8,128]{2,1,0:T(8,128)(2,1)S(1)}, u32[]{:S(2)}, u32[]{:S(2)}) %collective-permute-start.8) | collective-permute-done | bytes 409632 | tf_op jit(solution)/shard_map/ppermute | solution.py:292
  80.9 0.9 collective-permute-start.12
  81.8 0.3 collective-permute-start.7
  82.1 0.9 %widen.12.rest_0_ = f32[1280,1280]{1,0:T(8,128)} custom-call(s32[1]{0:T(128)} %bitcast.18.where, bf16[200,8,128]{2,1,0:T(8,128)(2,1)S(1)} %collective-permute-done.8.part, f32[1280,1280]{1,0:T(8,128)} %widen.11.rest_0_), custom_call_target="tpu_custom_call", output_to_operand_aliasing={{}: (2, {})} | custom-call | flops 1073741824 | bytes 1048576 | tf_op jit(solution)/shard_map/widen/pallas_call | solution.py:239
  83.0 0.1 collective-permute-done.12.part
  83.2 0.9 %widen.13.rest_0_ = f32[1280,1280]{1,0:T(8,128)} custom-call(s32[1]{0:T(128)} %bitcast.13.where, bf16[200,8,128]{2,1,0:T(8,128)(2,1)S(1)} %collective-permute-done.12.part, f32[1280,1280]{1,0:T(8,128)} %widen.12.rest_0_), custom_call_target="tpu_custom_call", output_to_operand_aliasing={{}: (2, {})} | custom-call | flops 1073741824 | bytes 1048576 | tf_op jit(solution)/shard_map/widen/pallas_call | solution.py:239
  84.1 6.0 %collective-permute-done.7.part = bf16[200,8,128]{2,1,0:T(8,128)(2,1)S(1)} collective-permute-done((bf16[200,8,128]{2,1,0:T(8,128)(2,1)S(1)}, bf16[200,8,128]{2,1,0:T(8,128)(2,1)S(1)}, u32[]{:S(2)}, u32[]{:S(2)}) %collective-permute-start.7) | collective-permute-done | bytes 409632 | tf_op jit(solution)/shard_map/ppermute | solution.py:292
  90.1 0.9 collective-permute-start.13
  91.0 0.9 %widen.14.rest_0_ = f32[1280,1280]{1,0:T(8,128)} custom-call(s32[1]{0:T(128)} %bitcast.19.where, bf16[200,8,128]{2,1,0:T(8,128)(2,1)S(1)} %collective-permute-done.7.part, f32[1280,1280]{1,0:T(8,128)} %widen.13.rest_0_), custom_call_target="tpu_custom_call", output_to_operand_aliasing={{}: (2, {})} | custom-call | flops 1073741824 | bytes 1048576 | tf_op jit(solution)/shard_map/widen/pallas_call | solution.py:239
  91.9 0.4 collective-permute-done.13.part
  92.3 0.9 %widen.15 = f32[1280,1280]{1,0:T(8,128)} custom-call(s32[1]{0:T(128)} %bitcast.where, bf16[200,8,128]{2,1,0:T(8,128)(2,1)S(1)} %collective-permute-done.13.part, f32[1280,1280]{1,0:T(8,128)} %widen.14.rest_0_), custom_call_target="tpu_custom_call", output_to_operand_aliasing={{}: (2, {})} | custom-call | flops 1073741824 | bytes 1048576 | tf_op jit(solution)/shard_map/widen/pallas_call | solution.py:239
  (1 shorter events, 0.0 us)
Async XLA Ops:
  0.1 0.9 copy-start
  14.2 2.8 %collective-permute-start.5 = (bf16[160,1280]{1,0:T(8,128)(2,1)S(1)}, bf16[160,1280]{1,0:T(8,128)(2,1)S(1)}, u32[]{:S(2)}, u32[]{:S(2)}) collective-permute-start(bf16[160,1280]{1,0:T(8,128)(2,1)S(1)} %get-tuple-element.21), channel_id=1, source_target_pairs={{0,32},{32,0},{1,33},{33,1},{2,34},{34,2},{3,35},{35,3},{4,36},{36... | collective-permute-start | bytes 1228808 | tf_op jit(solution)/shard_map/ppermute | solution.py:258
  15.7 4.4 %collective-permute-start.3 = (bf16[160,1280]{1,0:T(8,128)(2,1)S(1)}, bf16[160,1280]{1,0:T(8,128)(2,1)S(1)}, u32[]{:S(2)}, u32[]{:S(2)}) collective-permute-start(bf16[160,1280]{1,0:T(8,128)(2,1)S(1)} %get-tuple-element.22), channel_id=1, source_target_pairs={{0,32},{32,0},{1,33},{33,1},{2,34},{34,2},{3,35},{35,3},{4,36},{36... | collective-permute-start | bytes 1228808 | tf_op jit(solution)/shard_map/ppermute | solution.py:258
  15.8 4.5 %collective-permute-start.1 = (bf16[160,1280]{1,0:T(8,128)(2,1)S(1)}, bf16[160,1280]{1,0:T(8,128)(2,1)S(1)}, u32[]{:S(2)}, u32[]{:S(2)}) collective-permute-start(bf16[160,1280]{1,0:T(8,128)(2,1)S(1)} %get-tuple-element.23), channel_id=1, source_target_pairs={{0,32},{32,0},{1,33},{33,1},{2,34},{34,2},{3,35},{35,3},{4,36},{36... | collective-permute-start | bytes 1228808 | tf_op jit(solution)/shard_map/ppermute | solution.py:258
  16.2 5.9 %collective-permute-start = (bf16[160,1280]{1,0:T(8,128)(2,1)S(1)}, bf16[160,1280]{1,0:T(8,128)(2,1)S(1)}, u32[]{:S(2)}, u32[]{:S(2)}) collective-permute-start(bf16[160,1280]{1,0:T(8,128)(2,1)S(1)} %get-tuple-element.24), channel_id=1, source_target_pairs={{0,32},{32,0},{1,33},{33,1},{2,34},{34,2},{3,35},{35,3},{4,36},{36... | collective-permute-start | bytes 1228808 | tf_op jit(solution)/shard_map/ppermute | solution.py:258
  17.2 12.2 %collective-permute-start.6 = (bf16[160,1280]{1,0:T(8,128)(2,1)S(1)}, bf16[160,1280]{1,0:T(8,128)(2,1)S(1)}, u32[]{:S(2)}, u32[]{:S(2)}) collective-permute-start(bf16[160,1280]{1,0:T(8,128)(2,1)S(1)} %shard_map.49), channel_id=1, source_target_pairs={{0,3},{4,7},{8,11},{12,15},{16,19},{20,23},{24,27},{28,31},{64,67}... | collective-permute-start | bytes 1228808 | tf_op jit(solution)/shard_map/ppermute | solution.py:284
  20.2 12.8 %collective-permute-start.4 = (bf16[160,1280]{1,0:T(8,128)(2,1)S(1)}, bf16[160,1280]{1,0:T(8,128)(2,1)S(1)}, u32[]{:S(2)}, u32[]{:S(2)}) collective-permute-start(bf16[160,1280]{1,0:T(8,128)(2,1)S(1)} %shard_map.48), channel_id=1, source_target_pairs={{0,1},{4,5},{8,9},{12,13},{16,17},{20,21},{24,25},{28,29},{64,65},... | collective-permute-start | bytes 1228808 | tf_op jit(solution)/shard_map/ppermute | solution.py:284
  20.4 12.6 %collective-permute-start.2 = (bf16[160,1280]{1,0:T(8,128)(2,1)S(1)}, bf16[160,1280]{1,0:T(8,128)(2,1)S(1)}, u32[]{:S(2)}, u32[]{:S(2)}) collective-permute-start(bf16[160,1280]{1,0:T(8,128)(2,1)S(1)} %shard_map.47), channel_id=1, source_target_pairs={{0,2},{4,6},{8,10},{12,14},{16,18},{20,22},{24,26},{28,30},{64,66}... | collective-permute-start | bytes 1228808 | tf_op jit(solution)/shard_map/ppermute | solution.py:284
  61.5 4.6 %collective-permute-start.10 = (bf16[200,8,128]{2,1,0:T(8,128)(2,1)S(1)}, bf16[200,8,128]{2,1,0:T(8,128)(2,1)S(1)}, u32[]{:S(2)}, u32[]{:S(2)}) collective-permute-start(bf16[200,8,128]{2,1,0:T(8,128)(2,1)S(1)} %slice.20.part), channel_id=1, source_target_pairs={{0,32},{32,0},{1,33},{33,1},{2,34},{34,2},{3,35},{35,3},{4,36},{36... | collective-permute-start | bytes 1228808 | tf_op jit(solution)/shard_map/ppermute | solution.py:258
  64.3 8.6 %collective-permute-start.9 = (bf16[200,8,128]{2,1,0:T(8,128)(2,1)S(1)}, bf16[200,8,128]{2,1,0:T(8,128)(2,1)S(1)}, u32[]{:S(2)}, u32[]{:S(2)}) collective-permute-start(bf16[200,8,128]{2,1,0:T(8,128)(2,1)S(1)} %slice.20.part), channel_id=1, source_target_pairs={{2,0},{6,4},{10,8},{14,12},{18,16},{22,20},{26,24},{30,28},{66,64}... | collective-permute-start | bytes 1228808 | tf_op jit(solution)/shard_map/ppermute | solution.py:292
  72.9 2.5 %collective-permute-start.11 = (bf16[200,8,128]{2,1,0:T(8,128)(2,1)S(1)}, bf16[200,8,128]{2,1,0:T(8,128)(2,1)S(1)}, u32[]{:S(2)}, u32[]{:S(2)}) collective-permute-start(bf16[200,8,128]{2,1,0:T(8,128)(2,1)S(1)} %collective-permute-done.9.part), channel_id=1, source_target_pairs={{0,32},{32,0},{1,33},{33,1},{2,34},{34,2},{3,35},{35,3},{4,36},{36... | collective-permute-start | bytes 1228808 | tf_op jit(solution)/shard_map/ppermute | solution.py:258
  73.8 7.1 %collective-permute-start.8 = (bf16[200,8,128]{2,1,0:T(8,128)(2,1)S(1)}, bf16[200,8,128]{2,1,0:T(8,128)(2,1)S(1)}, u32[]{:S(2)}, u32[]{:S(2)}) collective-permute-start(bf16[200,8,128]{2,1,0:T(8,128)(2,1)S(1)} %slice.20.part), channel_id=1, source_target_pairs={{1,0},{5,4},{9,8},{13,12},{17,16},{21,20},{25,24},{29,28},{65,64},... | collective-permute-start | bytes 1228808 | tf_op jit(solution)/shard_map/ppermute | solution.py:292
  80.9 2.2 %collective-permute-start.12 = (bf16[200,8,128]{2,1,0:T(8,128)(2,1)S(1)}, bf16[200,8,128]{2,1,0:T(8,128)(2,1)S(1)}, u32[]{:S(2)}, u32[]{:S(2)}) collective-permute-start(bf16[200,8,128]{2,1,0:T(8,128)(2,1)S(1)} %collective-permute-done.8.part), channel_id=1, source_target_pairs={{0,32},{32,0},{1,33},{33,1},{2,34},{34,2},{3,35},{35,3},{4,36},{36... | collective-permute-start | bytes 1228808 | tf_op jit(solution)/shard_map/ppermute | solution.py:258
  81.8 8.3 %collective-permute-start.7 = (bf16[200,8,128]{2,1,0:T(8,128)(2,1)S(1)}, bf16[200,8,128]{2,1,0:T(8,128)(2,1)S(1)}, u32[]{:S(2)}, u32[]{:S(2)}) collective-permute-start(bf16[200,8,128]{2,1,0:T(8,128)(2,1)S(1)} %slice.20.part), channel_id=1, source_target_pairs={{3,0},{7,4},{11,8},{15,12},{19,16},{23,20},{27,24},{31,28},{67,64}... | collective-permute-start | bytes 1228808 | tf_op jit(solution)/shard_map/ppermute | solution.py:292
  90.1 2.2 %collective-permute-start.13 = (bf16[200,8,128]{2,1,0:T(8,128)(2,1)S(1)}, bf16[200,8,128]{2,1,0:T(8,128)(2,1)S(1)}, u32[]{:S(2)}, u32[]{:S(2)}) collective-permute-start(bf16[200,8,128]{2,1,0:T(8,128)(2,1)S(1)} %collective-permute-done.7.part), channel_id=1, source_target_pairs={{0,32},{32,0},{1,33},{33,1},{2,34},{34,2},{3,35},{35,3},{4,36},{36... | collective-permute-start | bytes 1228808 | tf_op jit(solution)/shard_map/ppermute | solution.py:258

commit v3 on v2

v3 whole, which is shorter than its diff:
```python
import functools

import jax
import jax.numpy as jnp
import numpy as np
from jax import lax
from jax.experimental import pallas as pl
from jax.experimental.pallas import tpu as pltpu
from jax.sharding import Mesh
from jax.sharding import PartitionSpec as P


D = 1280
BLOCK = 128
HALF = D // 2
COLS = D // BLOCK
AXES = ("zl", "c", "zh", "y", "x")
SIZES = (2, 2, 2, 4, 4)
QUARTER = HALF // 4
TILES = QUARTER // 8 * COLS
PER_CHIP = -(-TILES // 16)
OWNED = PER_CHIP * 8
CHUNK = 512
MROWS = 256
EARLY = 3
WSTEPS = 5
MIB = 1 << 20
GRANT = 34
ORDER = (2, 1, 3, 0)
WRITES = {
    "write_0": ((0, True), (0, False)),
    "write_1": ((1, True), (1, False)),
    "write_2": ((3, True),),
    "write_3": ((3, False), (2, True)),
    "write_4": ((2, False),),
}


def device(zl, c, zh, y, x):
    return int(np.ravel_multi_index((zl, c, zh, y, x), SIZES))


def line(core, lead):
    spots = [(zl, zh, o) for zl in range(2) for zh in range(2) for o in range(4)]
    if core == 0:
        return [device(zl, 0, zh, o, lead) for zl, zh, o in spots]
    return [device(zl, 1, zh, lead, o) for zl, zh, o in spots]


SIXTEENS = [line(core, lead) for core in range(2) for lead in range(4)]


def from_ahead(k):
    pairs = []
    for core in range(2):
        for lead in range(4):
            pairs += list(zip(line(core, (lead + k) % 4), line(core, lead)))
    return pairs


def to_ahead(k):
    return [(source, target) for target, source in from_ahead(k)]


def params(mib, **more):
    return pltpu.CompilerParams(vmem_limit_bytes=mib * MIB, **more)


def quantized(v):
    largest = jnp.max(jnp.abs(v), axis=-1, keepdims=True)
    scale = ((largest + 1e-06) / 127.0).astype(jnp.bfloat16).astype(jnp.float32)
    level = (v * (1.0 / scale)).astype(jnp.bfloat16).astype(jnp.float32)
    return level * scale


def piece_start(core, quarter):
    return quarter // 2 * HALF + core * (HALF // 2) + quarter % 2 * QUARTER


def piece_index(core, quarter):
    return quarter // 2 * 4 + core * 2 + quarter % 2


def multiplied(a, c):
    return lax.dot_general(a, c, (((0,), (0,)), ((), ())), preferred_element_type=jnp.float32)


def gradient_kernel(
    spot, act, cot, error, owner, v, early_v, late_v, cot_v, err, own, acc, early_sem, late_sem, cot_sem, err_sem, own_sem
):
    chunks = cot.shape[0] // CHUNK
    blocks = D // MROWS

    def slab(i):
        return pl.ds(i * CHUNK, CHUNK)

    def early(i):
        return (
            pltpu.make_async_copy(
                act.at[slab(i), pl.ds(0, EARLY * MROWS)], early_v.at[slab(i), :], early_sem.at[i]
            ),
            pltpu.make_async_copy(cot.at[slab(i), :], cot_v.at[slab(i), :], cot_sem.at[i]),
        )

    def late(j):
        return pltpu.make_async_copy(
            act.at[:, pl.ds(j * MROWS, MROWS)], late_v.at[j - EARLY], late_sem.at[j - EARLY]
        )

    def load_err(j):
        at = pl.ds(j * MROWS, MROWS)
        return pltpu.make_async_copy(error.at[at, :], err.at[at, :], err_sem.at[j])

    def finish(j):
        at = slice(j * MROWS, (j + 1) * MROWS)
        for b in range(0, D, BLOCK):
            cols = slice(b, b + BLOCK)
            v[at, cols] = quantized(acc[at, cols] + err[at, cols])

    load_own = pltpu.make_async_copy(owner, own, own_sem)
    for i in range(2):
        for copy in early(i):
            copy.start()
    for i in range(chunks):
        for copy in early(i):
            copy.wait()
        if i + 2 < chunks:
            for copy in early(i + 2):
                copy.start()
        elif i + 2 == chunks:
            late(EARLY).start()
            for j in range(blocks):
                load_err(j).start()
                if EARLY < j + EARLY + 1 < blocks:
                    late(j + EARLY + 1).start()
            load_own.start()
        for j in range(EARLY):
            at = slice(j * MROWS, (j + 1) * MROWS)
            product = multiplied(early_v[i * CHUNK : (i + 1) * CHUNK, at], cot_v[i * CHUNK : (i + 1) * CHUNK, :])
            acc[at, :] = product if i == 0 else acc[at, :] + product
    done = 0
    for j in range(EARLY, blocks):
        late(j).wait()
        ready = j if j + 1 == blocks else min(j, done + 2 if j > EARLY else 1)
        for q in range(done, ready):
            load_err(q).wait()
        acc[j * MROWS : (j + 1) * MROWS, :] = multiplied(late_v[j - EARLY], cot_v[...])
        for q in range(done, ready):
            finish(q)
        done = ready
    load_own.wait()
    for q in range(done, blocks):
        load_err(q).wait()
        finish(q)
    row = spot[0]
    for shift in (0, 2, 4, 6):

        @pl.when(row % 8 == shift)
        def _():
            for i in range(2):
                low, high = max(shift - 8 * i, 0), min(shift + 10 - 8 * i, 8)
                rows = pl.ds(pl.multiple_of(row // 8 * 8 + 8 * i, 8), 8)
                mine = own[low - shift + 8 * i : high - shift + 8 * i, :]
                v[rows, :] = v[rows, :] + jnp.pad(mine, ((low, 8 - high), (0, 0)))


def gradient(spot, act, cot, error, owner):
    tokens = act.shape[0]
    hbm, vmem = pl.BlockSpec(memory_space=pltpu.HBM), pl.BlockSpec(memory_space=pltpu.VMEM)
    blocks, chunks = D // MROWS, tokens // CHUNK
    return pl.pallas_call(
        gradient_kernel,
        out_shape=pltpu.VMEM((D, D), jnp.float32),
        in_specs=[pl.BlockSpec(memory_space=pltpu.SMEM)] + [hbm] * 4,
        out_specs=vmem,
        scratch_shapes=[
            pltpu.VMEM((tokens, EARLY * MROWS), jnp.bfloat16),
            pltpu.VMEM((blocks - EARLY, tokens, MROWS), jnp.bfloat16),
            pltpu.VMEM((tokens, D), jnp.bfloat16),
            pltpu.VMEM((D, D), jnp.float32),
            pltpu.VMEM(owner.shape, jnp.float32),
            pltpu.VMEM((D, D), jnp.float32),
            pltpu.SemaphoreType.DMA((chunks,)),
            pltpu.SemaphoreType.DMA((blocks - EARLY,)),
            pltpu.SemaphoreType.DMA((chunks,)),
            pltpu.SemaphoreType.DMA((blocks,)),
            pltpu.SemaphoreType.DMA,
        ],
        compiler_params=params(GRANT),
        cost_estimate=pl.CostEstimate(
            flops=2 * tokens * D * D, bytes_accessed=17 * MIB, transcendentals=0
        ),
        name="gradient",
    )(spot, act, cot, error, owner)


def multiplied(a, c):
    return lax.dot_general(a, c, (((0,), (0,)), ((), ())), preferred_element_type=jnp.float32)


def pick_kernel(core, lead, v, *outs):
    for k, out in enumerate(outs):
        start = piece_start(core[0], (lead[0] + k) % 4)
        out[...] = v[pl.ds(pl.multiple_of(start, 32), QUARTER), :].astype(out.dtype)


def pick(core, lead, v):
    smem, vmem = pl.BlockSpec(memory_space=pltpu.SMEM), pl.BlockSpec(memory_space=pltpu.VMEM)
    return pl.pallas_call(
        pick_kernel,
        out_shape=[jax.ShapeDtypeStruct((QUARTER, D), jnp.bfloat16)] * 4,
        in_specs=[smem, smem, vmem],
        out_specs=[vmem] * 4,
        compiler_params=params(4),
        cost_estimate=pl.CostEstimate(flops=1 << 28, bytes_accessed=2 * MIB, transcendentals=0),
        name="pick",
    )(core, lead, v)


def pair_kernel(k, core, lead, v, got, out):
    start = piece_start(core[0], (lead[0] + k) % 4)
    kept = v[pl.ds(pl.multiple_of(start, 32), QUARTER), :]
    out[...] = (kept + got[...].astype(jnp.float32)).astype(out.dtype)


def pair(core, lead, v, got, k):
    smem, vmem = pl.BlockSpec(memory_space=pltpu.SMEM), pl.BlockSpec(memory_space=pltpu.VMEM)
    return pl.pallas_call(
        functools.partial(pair_kernel, k),
        out_shape=jax.ShapeDtypeStruct((QUARTER, D), jnp.bfloat16 if k else jnp.float32),
        in_specs=[smem, smem, vmem, vmem],
        out_specs=vmem,
        compiler_params=params(4),
        cost_estimate=pl.CostEstimate(flops=1 << 28, bytes_accessed=2 * MIB, transcendentals=0),
    )(core, lead, v, got)


def total_kernel(own, *rest):
    out = rest[-1]
    for b in range(COLS):
        at = slice(b * BLOCK, (b + 1) * BLOCK)
        total = own[:, at]
        for got in rest[:-1]:
            total = total + got[:, at].astype(jnp.float32)
        total = total.astype(jnp.bfloat16).reshape(QUARTER // 8, 8, BLOCK)
        for r in range(QUARTER // 8):
            out[r * COLS + b] = total[r]
    out[TILES:] = jnp.zeros_like(out[TILES:])


def total_of(own, *others):
    return pl.pallas_call(
        total_kernel,
        out_shape=jax.ShapeDtypeStruct((16 * PER_CHIP, 8, BLOCK), jnp.bfloat16),
        in_specs=[pl.BlockSpec(memory_space=pltpu.VMEM)] * (1 + len(others)),
        out_specs=pl.BlockSpec(memory_space=pltpu.VMEM),
        compiler_params=params(4),
        cost_estimate=pl.CostEstimate(flops=4 * QUARTER * D, bytes_accessed=2 * MIB, transcendentals=0),
        name="total",
    )(own, *others)


def owner_kernel(parts, out):
    total = parts[0].astype(jnp.float32)
    for k in range(1, parts.shape[0]):
        total = total + parts[k].astype(jnp.float32)
    update = quantized(total).astype(jnp.bfloat16)
    for k in range(out.shape[0]):
        out[k] = update


def owner_update(parts):
    return pl.pallas_call(
        owner_kernel,
        out_shape=jax.ShapeDtypeStruct((16, OWNED, BLOCK), jnp.bfloat16),
        in_specs=[pl.BlockSpec(memory_space=pltpu.VMEM)],
        out_specs=pl.BlockSpec(memory_space=pltpu.VMEM),
        compiler_params=params(8),
        cost_estimate=pl.CostEstimate(
            flops=parts.size, bytes_accessed=2 * MIB, transcendentals=0
        ),
        name="owner",
    )(parts)


def widen_kernel(count, *refs):
    indices, parts = refs[:count], refs[count : 2 * count]
    out, wide, sem = refs[-3:]
    rows = QUARTER // WSTEPS

    def copy(n, i):
        start = indices[n][0] * QUARTER + i * rows
        return pltpu.make_async_copy(
            wide.at[n, pl.ds(i * rows, rows), :],
            out.at[pl.ds(pl.multiple_of(start, 8), rows), :],
            sem.at[n, i],
        )

    for n, part in enumerate(parts):
        for i in range(WSTEPS):
            for r in range(i * rows // 8, (i + 1) * rows // 8):
                for b in range(COLS):
                    wide[n, r * 8 : r * 8 + 8, b * BLOCK : (b + 1) * BLOCK] = part[
                        r * COLS + b
                    ].astype(jnp.float32)
            copy(n, i).start()
    for n in range(count):
        for i in range(WSTEPS):
            copy(n, i).wait()


def widen(indices, parts, base):
    count = len(parts)
    smem, vmem = pl.BlockSpec(memory_space=pltpu.SMEM), pl.BlockSpec(memory_space=pltpu.VMEM)
    specs = [smem] * count + [vmem] * count
    args = [*indices, *parts]
    aliases = {}
    if base is not None:
        specs.append(pl.BlockSpec(memory_space=pltpu.HBM))
        args.append(base)
        aliases = {2 * count: 0}
    return pl.pallas_call(
        functools.partial(widen_kernel, count),
        out_shape=pltpu.HBM((D, D), jnp.float32),
        in_specs=specs,
        out_specs=pl.BlockSpec(memory_space=pltpu.HBM),
        scratch_shapes=[
            pltpu.VMEM((count, QUARTER, D), jnp.float32),
            pltpu.SemaphoreType.DMA((count, WSTEPS)),
        ],
        input_output_aliases=aliases,
        compiler_params=params(4),
        cost_estimate=pl.CostEstimate(flops=1 << 30, bytes_accessed=MIB, transcendentals=0),
        name="widen",
    )(*args)


def swap_cores(value):
    return lax.ppermute(value, "c", [(0, 1), (1, 0)])


def one(value):
    return value.astype(jnp.int32).reshape(1)


def on_device(activations, cotangent, carried_error, owner_error):
    core = lax.axis_index("c")
    x, y = lax.axis_index("x"), lax.axis_index("y")
    lead = jnp.where(core == 0, x, y)
    other_lead = x + y - lead
    spot = one(lax.axis_index(AXES) * owner_error.shape[0])
    error = carried_error.reshape(D, D)
    args = (activations, cotangent, error, owner_error)
    args = [pltpu.with_memory_space_constraint(v, pltpu.HBM) for v in args]
    v = gradient(spot, *args)
    sent = pick(one(1 - core), one(other_lead), v)
    got = {}
    for k in ORDER:
        got[k] = swap_cores(sent[k])
    arrived = []
    for k in ORDER:
        piece = pair(one(core), one(lead), v, got[k], k)
        if k:
            piece = lax.ppermute(piece, AXES, to_ahead(k))
        arrived.append(piece)
    parts = total_of(*arrived[::-1]).reshape(16, OWNED, BLOCK)
    parts = lax.all_to_all(parts, AXES, 0, 0, axis_index_groups=SIXTEENS, tiled=True)
    update = owner_update(parts)
    mine = lax.all_to_all(update, AXES, 0, 0, axis_index_groups=SIXTEENS, tiled=True)
    pieces = {0: mine.reshape(16 * PER_CHIP, 8, BLOCK)[:TILES]}
    for k in (1, 3, 2):
        pieces[k] = lax.ppermute(pieces[0], AXES, from_ahead(k))
    theirs = {}
    for k in (0, 1, 3, 2):
        theirs[k] = swap_cores(pieces[k])
    out = None
    for parts in WRITES.values():
        indices = [
            one(piece_index(core, (lead + k) % 4))
            if own
            else one(piece_index(1 - core, (other_lead + k) % 4))
            for k, own in parts
        ]
        parts = [pieces[k] if own else theirs[k] for k, own in parts]
        out = widen(indices, parts, out)
    return out


def solution(mesh):
    fine = Mesh(mesh.devices.reshape(SIZES), AXES)
    return jax.shard_map(
        on_device,
        mesh=fine,
        in_specs=(P(AXES, None), P(AXES, None), P(AXES, None, None), P(AXES, None)),
        out_specs=P(),
        check_vma=False,
    )
```

time: 93.5 us -> 81.5 us (0.87)
  waiting for transfers between devices: 28.6 us -> 14.8 us
  starting transfers between devices: 14 us -> 21.2 us
  Pallas kernels: 21.4 us -> 17.9 us
  local copies, waits for them, and re-layouts: 1.02 us -> 0.03 us
    ppermute x6, waiting for transfers between devices: 27.2 us -> 14 us  [the longest x3 7.29 us: on_device(): piece = lax.ppermute(piece, AXES, to_ahead(k))]
    ppermute x6, starting transfers between devices: 6.4 us -> 10.1 us  [the longest x3 5.92 us: on_device(): piece = lax.ppermute(piece, AXES, to_ahead(k))]
    pallas_call x13 -> x11, Pallas kernels: 21.1 us -> 17.5 us  [the longest x1 11.3 us: gradient(): pl.pallas_call(gradient_kernel, out_shape=pltpu.VMEM((D, D), jnp.float32)...]
    ppermute x8, starting transfers between devices: 7.56 us -> 11.1 us  [swap_cores(): return lax.ppermute(value, 'c', [(0, 1), (1, 0)])]
  transfers between devices with their start and end apart: 14 -> 14, of which waited for: 8 -> 6; matrix products, arithmetic and copies ran while one was open for 0% -> 0% of each run, Pallas kernels for 7% -> 6%
where the time goes in v3:
time: 81.5 us; the launch traced here: 81.3 us
  blocking collectives  27.2 us (33%)
  starting transfers between devices  21.2 us (26%)
  Pallas kernels  17.9 us (22%)
  waiting for transfers between devices  14.8 us (18%)
    all_to_all x1, blocking collectives, on_device(): lax.all_to_all(parts, AXES, 0, 0, axis_index_groups=SIXTEENS, tiled=True)  16 us
    pallas_call x1, Pallas kernels, gradient(): pl.pallas_call(gradient_kernel, out_shape=pltpu.VMEM((D, D), jnp.float32)...  11.3 us
    all_to_all x1, blocking collectives, on_device(): lax.all_to_all(update, AXES, 0, 0, axis_index_groups=SIXTEENS, tiled=True)  11.2 us
    ppermute x8, starting transfers between devices, swap_cores(): return lax.ppermute(value, 'c', [(0, 1), (1, 0)])  11.1 us
    ppermute x3, waiting for transfers between devices, on_device(): piece = lax.ppermute(piece, AXES, to_ahead(k))  7.29 us
    ppermute x3, waiting for transfers between devices, on_device(): pieces[k] = lax.ppermute(pieces[0], AXES, from_ahead(k))  6.7 us
    ppermute x3, starting transfers between devices, on_device(): piece = lax.ppermute(piece, AXES, to_ahead(k))  5.92 us
    pallas_call x5, Pallas kernels, widen(): pl.pallas_call(functools.partial(widen_kernel, count), out_shape=pltpu.HB...  5.64 us
  transfers between devices with their start and end apart: 14, of which 6 were waited for; matrix products, arithmetic and copies ran while one was open for 0% of the time, Pallas kernels for 6%

profile of v3, /device:TPU:1, one launch (start us, length us, event | category | flops | bytes accessed | tf_op | source)
XLA Modules:
  0.0 81.3 jit_solution(17289614804128457363)
XLA Ops:
  0.0 11.3 %gradient.1.v = f32[1280,1280]{1,0:T(8,128)S(1)} custom-call(s32[1]{0:T(128)} %bitcast.3.spot, bf16[2048,1280]{1,0:T(8,128)(2,1)} %act.1, bf16[2048,1280]{1,0:T(8,128)(2,1)} %cot.1, f32[1280,1280]{1,0:T(8,128)} %bitcast.18, f32[10,1280]{1,0:T(8,128)} %owner.2), custom_call_target="tpu_custom_call" | custom-call | flops 6710886400 | bytes 17825792 | tf_op jit(solution)/shard_map/gradient/pallas_call | solution.py:171
  11.3 0.2 pick.1
  11.5 1.5 %collective-permute-start.5 = (bf16[160,1280]{1,0:T(8,128)(2,1)S(1)}, bf16[160,1280]{1,0:T(8,128)(2,1)S(1)}, u32[]{:S(2)}, u32[]{:S(2)}) collective-permute-start(bf16[160,1280]{1,0:T(8,128)(2,1)S(1)} %get-tuple-element.12), channel_id=1, source_target_pairs={{0,32},{32,0},{1,33},{33,1},{2,34},{34,2},{3,35},{35,3},{4,36},{36... | collective-permute-start | bytes 1228808 | tf_op jit(solution)/shard_map/ppermute | solution.py:339
  13.0 0.1 collective-permute-start.3
  13.1 0.4 collective-permute-start.1
  13.5 0.1 collective-permute-start
  13.6 0.8 collective-permute-done.5.got
  14.4 0.1 shard_map.49
  14.5 3.1 %collective-permute-start.6 = (bf16[160,1280]{1,0:T(8,128)(2,1)S(1)}, bf16[160,1280]{1,0:T(8,128)(2,1)S(1)}, u32[]{:S(2)}, u32[]{:S(2)}) collective-permute-start(bf16[160,1280]{1,0:T(8,128)(2,1)S(1)} %shard_map.49), channel_id=1, source_target_pairs={{0,2},{4,6},{8,10},{12,14},{16,18},{20,22},{24,26},{28,30},{64,66}... | collective-permute-start | bytes 1228808 | tf_op jit(solution)/shard_map/ppermute | solution.py:364
  17.6 0.0 collective-permute-done.3.got
  17.6 0.1 shard_map.48
  17.7 0.5 collective-permute-start.4
  18.1 0.0 collective-permute-done.1.got
  18.1 0.1 shard_map.47
  18.2 2.3 %collective-permute-start.2 = (bf16[160,1280]{1,0:T(8,128)(2,1)S(1)}, bf16[160,1280]{1,0:T(8,128)(2,1)S(1)}, u32[]{:S(2)}, u32[]{:S(2)}) collective-permute-start(bf16[160,1280]{1,0:T(8,128)(2,1)S(1)} %shard_map.47), channel_id=1, source_target_pairs={{0,3},{4,7},{8,11},{12,15},{16,19},{20,23},{24,27},{28,31},{64,67}... | collective-permute-start | bytes 1228808 | tf_op jit(solution)/shard_map/ppermute | solution.py:364
  20.6 0.0 collective-permute-done.got
  20.6 0.1 shard_map.46.own
  20.7 2.5 %collective-permute-done.6.rest_2_ = bf16[160,1280]{1,0:T(8,128)(2,1)S(1)} collective-permute-done((bf16[160,1280]{1,0:T(8,128)(2,1)S(1)}, bf16[160,1280]{1,0:T(8,128)(2,1)S(1)}, u32[]{:S(2)}, u32[]{:S(2)}) %collective-permute-start.6) | collective-permute-done | bytes 409632 | tf_op jit(solution)/shard_map/ppermute | solution.py:364
  23.2 4.4 %collective-permute-done.4.rest_1_ = bf16[160,1280]{1,0:T(8,128)(2,1)S(1)} collective-permute-done((bf16[160,1280]{1,0:T(8,128)(2,1)S(1)}, bf16[160,1280]{1,0:T(8,128)(2,1)S(1)}, u32[]{:S(2)}, u32[]{:S(2)}) %collective-permute-start.4) | collective-permute-done | bytes 409632 | tf_op jit(solution)/shard_map/ppermute | solution.py:364
  27.6 0.4 collective-permute-done.2.rest_0_
  28.0 0.2 total.1
  28.2 16.0 %all_to_all.10.parts = bf16[16,104,128]{2,1,0:T(8,128)(2,1)S(1)} all-to-all(bf16[16,104,128]{2,1,0:T(8,128)(2,1)S(1)} %bitcast.16), channel_id=1, replica_groups={{0,4,8,12,16,20,24,28,64,68,72,76,80,84,88,92},{1,5,9,13,17,21,25,29,65..., dimensions={0} | all-to-all | bytes 851968 | tf_op jit(solution)/shard_map/all_to_all | solution.py:367
  44.2 0.2 owner.3
  44.3 11.2 %all_to_all.11 = bf16[16,104,128]{2,1,0:T(8,128)(2,1)S(1)} all-to-all(bf16[16,104,128]{2,1,0:T(8,128)(2,1)S(1)} %owner.3), channel_id=1, replica_groups={{0,4,8,12,16,20,24,28,64,68,72,76,80,84,88,92},{1,5,9,13,17,21,25,29,65..., dimensions={0} | all-to-all | bytes 851968 | tf_op jit(solution)/shard_map/all_to_all | solution.py:369
  55.6 2.9 %collective-permute-start.11 = (bf16[200,8,128]{2,1,0:T(8,128)(2,1)S(1)}, bf16[200,8,128]{2,1,0:T(8,128)(2,1)S(1)}, u32[]{:S(2)}, u32[]{:S(2)}) collective-permute-start(bf16[200,8,128]{2,1,0:T(8,128)(2,1)S(1)} %slice.4.refs_2_), channel_id=1, source_target_pairs={{1,0},{5,4},{9,8},{13,12},{17,16},{21,20},{25,24},{29,28},{65,64},... | collective-permute-start | bytes 1228808 | tf_op jit(solution)/shard_map/ppermute | solution.py:372
  58.5 0.0 collective-permute-start.9
  58.5 1.3 %collective-permute-start.7 = (bf16[200,8,128]{2,1,0:T(8,128)(2,1)S(1)}, bf16[200,8,128]{2,1,0:T(8,128)(2,1)S(1)}, u32[]{:S(2)}, u32[]{:S(2)}) collective-permute-start(bf16[200,8,128]{2,1,0:T(8,128)(2,1)S(1)} %slice.4.refs_2_), channel_id=1, source_target_pairs={{2,0},{6,4},{10,8},{14,12},{18,16},{22,20},{26,24},{30,28},{66,64}... | collective-permute-start | bytes 1228808 | tf_op jit(solution)/shard_map/ppermute | solution.py:372
  59.7 4.3 %collective-permute-start.13 = (bf16[200,8,128]{2,1,0:T(8,128)(2,1)S(1)}, bf16[200,8,128]{2,1,0:T(8,128)(2,1)S(1)}, u32[]{:S(2)}, u32[]{:S(2)}) collective-permute-start(bf16[200,8,128]{2,1,0:T(8,128)(2,1)S(1)} %slice.4.refs_2_), channel_id=1, source_target_pairs={{0,32},{32,0},{1,33},{33,1},{2,34},{34,2},{3,35},{35,3},{4,36},{36... | collective-permute-start | bytes 1228808 | tf_op jit(solution)/shard_map/ppermute | solution.py:339
  64.1 3.7 %collective-permute-done.11.refs_2_ = bf16[200,8,128]{2,1,0:T(8,128)(2,1)S(1)} collective-permute-done((bf16[200,8,128]{2,1,0:T(8,128)(2,1)S(1)}, bf16[200,8,128]{2,1,0:T(8,128)(2,1)S(1)}, u32[]{:S(2)}, u32[]{:S(2)}) %collective-permute-start.11) | collective-permute-done | bytes 409632 | tf_op jit(solution)/shard_map/ppermute | solution.py:372
  67.8 0.4 collective-permute-start.12
  68.2 3.0 %collective-permute-done.9.refs_1_ = bf16[200,8,128]{2,1,0:T(8,128)(2,1)S(1)} collective-permute-done((bf16[200,8,128]{2,1,0:T(8,128)(2,1)S(1)}, bf16[200,8,128]{2,1,0:T(8,128)(2,1)S(1)}, u32[]{:S(2)}, u32[]{:S(2)}) %collective-permute-start.9) | collective-permute-done | bytes 409632 | tf_op jit(solution)/shard_map/ppermute | solution.py:372
  71.2 4.3 %collective-permute-start.10 = (bf16[200,8,128]{2,1,0:T(8,128)(2,1)S(1)}, bf16[200,8,128]{2,1,0:T(8,128)(2,1)S(1)}, u32[]{:S(2)}, u32[]{:S(2)}) collective-permute-start(bf16[200,8,128]{2,1,0:T(8,128)(2,1)S(1)} %collective-permute-done.9.refs_1_), channel_id=1, source_target_pairs={{0,32},{32,0},{1,33},{33,1},{2,34},{34,2},{3,35},{35,3},{4,36},{36... | collective-permute-start | bytes 1228808 | tf_op jit(solution)/shard_map/ppermute | solution.py:339
  75.4 0.0 collective-permute-done.7.refs_3_
  75.4 0.0 collective-permute-start.8
  75.5 0.0 collective-permute-done.13.refs_3_
  75.5 1.3 %widen.5.refs_4_ = f32[1280,1280]{1,0:T(8,128)} custom-call(s32[1]{0:T(128)} %bitcast.14.refs_0_, s32[1]{0:T(128)} %bitcast.15.refs_1_, bf16[200,8,128]{2,1,0:T(8,128)(2,1)S(1)} %slice.4.refs_2_, bf16[200,8,128]{2,1,0:T(8,128)(2,1)S(1)} %collective-permute-done.13.refs_3_), custom_call_target="tpu_custom_call" | custom-call | flops 1073741824 | bytes 1048576 | tf_op jit(solution)/shard_map/widen/pallas_call | solution.py:322
  76.7 0.0 collective-permute-done.12.refs_3_
  76.7 1.3 %widen.6.refs_2_ = f32[1280,1280]{1,0:T(8,128)} custom-call(s32[1]{0:T(128)} %bitcast.12.refs_0_, s32[1]{0:T(128)} %bitcast.13.refs_1_, bf16[200,8,128]{2,1,0:T(8,128)(2,1)S(1)} %collective-permute-done.11.refs_2_, bf16[200,8,128]{2,1,0:T(8,128)(2,1)S(1)} %collective-permute-done.12.refs_3_, f32[1280,1280]{1,0:T(8,128)} %widen.5.refs_4_), custom_call_target="tpu_custom_call", output_to_operand_aliasing={{}: (4, {})} | custom-call | flops 1073741824 | bytes 1048576 | tf_op jit(solution)/shard_map/widen/pallas_call | solution.py:322
  78.0 0.9 %widen.7.refs_4_ = f32[1280,1280]{1,0:T(8,128)} custom-call(s32[1]{0:T(128)} %bitcast.11.refs_0_, bf16[200,8,128]{2,1,0:T(8,128)(2,1)S(1)} %collective-permute-done.9.refs_1_, f32[1280,1280]{1,0:T(8,128)} %widen.6.refs_2_), custom_call_target="tpu_custom_call", output_to_operand_aliasing={{}: (2, {})} | custom-call | flops 1073741824 | bytes 1048576 | tf_op jit(solution)/shard_map/widen/pallas_call | solution.py:322
  78.9 0.0 collective-permute-done.10.refs_2_
  78.9 1.3 %widen.8.refs_2_ = f32[1280,1280]{1,0:T(8,128)} custom-call(s32[1]{0:T(128)} %bitcast.9.refs_0_, s32[1]{0:T(128)} %bitcast.10.refs_1_, bf16[200,8,128]{2,1,0:T(8,128)(2,1)S(1)} %collective-permute-done.10.refs_2_, bf16[200,8,128]{2,1,0:T(8,128)(2,1)S(1)} %collective-permute-done.7.refs_3_, f32[1280,1280]{1,0:T(8,128)} %widen.7.refs_4_), custom_call_target="tpu_custom_call", output_to_operand_aliasing={{}: (4, {})} | custom-call | flops 1073741824 | bytes 1048576 | tf_op jit(solution)/shard_map/widen/pallas_call | solution.py:322
  80.2 0.0 collective-permute-done.8.refs_1_
  80.2 0.9 %widen.9 = f32[1280,1280]{1,0:T(8,128)} custom-call(s32[1]{0:T(128)} %bitcast.refs_0_, bf16[200,8,128]{2,1,0:T(8,128)(2,1)S(1)} %collective-permute-done.8.refs_1_, f32[1280,1280]{1,0:T(8,128)} %widen.8.refs_2_), custom_call_target="tpu_custom_call", output_to_operand_aliasing={{}: (2, {})} | custom-call | flops 1073741824 | bytes 1048576 | tf_op jit(solution)/shard_map/widen/pallas_call | solution.py:322
  (1 shorter events, 0.0 us)
Async XLA Ops:
  11.5 2.8 %collective-permute-start.5 = (bf16[160,1280]{1,0:T(8,128)(2,1)S(1)}, bf16[160,1280]{1,0:T(8,128)(2,1)S(1)}, u32[]{:S(2)}, u32[]{:S(2)}) collective-permute-start(bf16[160,1280]{1,0:T(8,128)(2,1)S(1)} %get-tuple-element.12), channel_id=1, source_target_pairs={{0,32},{32,0},{1,33},{33,1},{2,34},{34,2},{3,35},{35,3},{4,36},{36... | collective-permute-start | bytes 1228808 | tf_op jit(solution)/shard_map/ppermute | solution.py:339
  13.0 4.6 %collective-permute-start.3 = (bf16[160,1280]{1,0:T(8,128)(2,1)S(1)}, bf16[160,1280]{1,0:T(8,128)(2,1)S(1)}, u32[]{:S(2)}, u32[]{:S(2)}) collective-permute-start(bf16[160,1280]{1,0:T(8,128)(2,1)S(1)} %get-tuple-element.11), channel_id=1, source_target_pairs={{0,32},{32,0},{1,33},{33,1},{2,34},{34,2},{3,35},{35,3},{4,36},{36... | collective-permute-start | bytes 1228808 | tf_op jit(solution)/shard_map/ppermute | solution.py:339
  13.1 5.1 %collective-permute-start.1 = (bf16[160,1280]{1,0:T(8,128)(2,1)S(1)}, bf16[160,1280]{1,0:T(8,128)(2,1)S(1)}, u32[]{:S(2)}, u32[]{:S(2)}) collective-permute-start(bf16[160,1280]{1,0:T(8,128)(2,1)S(1)} %get-tuple-element.10), channel_id=1, source_target_pairs={{0,32},{32,0},{1,33},{33,1},{2,34},{34,2},{3,35},{35,3},{4,36},{36... | collective-permute-start | bytes 1228808 | tf_op jit(solution)/shard_map/ppermute | solution.py:339
  13.5 7.1 %collective-permute-start = (bf16[160,1280]{1,0:T(8,128)(2,1)S(1)}, bf16[160,1280]{1,0:T(8,128)(2,1)S(1)}, u32[]{:S(2)}, u32[]{:S(2)}) collective-permute-start(bf16[160,1280]{1,0:T(8,128)(2,1)S(1)} %get-tuple-element.9), channel_id=1, source_target_pairs={{0,32},{32,0},{1,33},{33,1},{2,34},{34,2},{3,35},{35,3},{4,36},{36... | collective-permute-start | bytes 1228808 | tf_op jit(solution)/shard_map/ppermute | solution.py:339
  14.5 8.7 %collective-permute-start.6 = (bf16[160,1280]{1,0:T(8,128)(2,1)S(1)}, bf16[160,1280]{1,0:T(8,128)(2,1)S(1)}, u32[]{:S(2)}, u32[]{:S(2)}) collective-permute-start(bf16[160,1280]{1,0:T(8,128)(2,1)S(1)} %shard_map.49), channel_id=1, source_target_pairs={{0,2},{4,6},{8,10},{12,14},{16,18},{20,22},{24,26},{28,30},{64,66}... | collective-permute-start | bytes 1228808 | tf_op jit(solution)/shard_map/ppermute | solution.py:364
  17.7 9.9 %collective-permute-start.4 = (bf16[160,1280]{1,0:T(8,128)(2,1)S(1)}, bf16[160,1280]{1,0:T(8,128)(2,1)S(1)}, u32[]{:S(2)}, u32[]{:S(2)}) collective-permute-start(bf16[160,1280]{1,0:T(8,128)(2,1)S(1)} %shard_map.48), channel_id=1, source_target_pairs={{0,1},{4,5},{8,9},{12,13},{16,17},{20,21},{24,25},{28,29},{64,65},... | collective-permute-start | bytes 1228808 | tf_op jit(solution)/shard_map/ppermute | solution.py:364
  18.2 9.7 %collective-permute-start.2 = (bf16[160,1280]{1,0:T(8,128)(2,1)S(1)}, bf16[160,1280]{1,0:T(8,128)(2,1)S(1)}, u32[]{:S(2)}, u32[]{:S(2)}) collective-permute-start(bf16[160,1280]{1,0:T(8,128)(2,1)S(1)} %shard_map.47), channel_id=1, source_target_pairs={{0,3},{4,7},{8,11},{12,15},{16,19},{20,23},{24,27},{28,31},{64,67}... | collective-permute-start | bytes 1228808 | tf_op jit(solution)/shard_map/ppermute | solution.py:364
  55.6 12.2 %collective-permute-start.11 = (bf16[200,8,128]{2,1,0:T(8,128)(2,1)S(1)}, bf16[200,8,128]{2,1,0:T(8,128)(2,1)S(1)}, u32[]{:S(2)}, u32[]{:S(2)}) collective-permute-start(bf16[200,8,128]{2,1,0:T(8,128)(2,1)S(1)} %slice.4.refs_2_), channel_id=1, source_target_pairs={{1,0},{5,4},{9,8},{13,12},{17,16},{21,20},{25,24},{29,28},{65,64},... | collective-permute-start | bytes 1228808 | tf_op jit(solution)/shard_map/ppermute | solution.py:372
  58.5 12.7 %collective-permute-start.9 = (bf16[200,8,128]{2,1,0:T(8,128)(2,1)S(1)}, bf16[200,8,128]{2,1,0:T(8,128)(2,1)S(1)}, u32[]{:S(2)}, u32[]{:S(2)}) collective-permute-start(bf16[200,8,128]{2,1,0:T(8,128)(2,1)S(1)} %slice.4.refs_2_), channel_id=1, source_target_pairs={{3,0},{7,4},{11,8},{15,12},{19,16},{23,20},{27,24},{31,28},{67,64}... | collective-permute-start | bytes 1228808 | tf_op jit(solution)/shard_map/ppermute | solution.py:372
  58.5 17.0 %collective-permute-start.7 = (bf16[200,8,128]{2,1,0:T(8,128)(2,1)S(1)}, bf16[200,8,128]{2,1,0:T(8,128)(2,1)S(1)}, u32[]{:S(2)}, u32[]{:S(2)}) collective-permute-start(bf16[200,8,128]{2,1,0:T(8,128)(2,1)S(1)} %slice.4.refs_2_), channel_id=1, source_target_pairs={{2,0},{6,4},{10,8},{14,12},{18,16},{22,20},{26,24},{30,28},{66,64}... | collective-permute-start | bytes 1228808 | tf_op jit(solution)/shard_map/ppermute | solution.py:372
  59.7 15.7 %collective-permute-start.13 = (bf16[200,8,128]{2,1,0:T(8,128)(2,1)S(1)}, bf16[200,8,128]{2,1,0:T(8,128)(2,1)S(1)}, u32[]{:S(2)}, u32[]{:S(2)}) collective-permute-start(bf16[200,8,128]{2,1,0:T(8,128)(2,1)S(1)} %slice.4.refs_2_), channel_id=1, source_target_pairs={{0,32},{32,0},{1,33},{33,1},{2,34},{34,2},{3,35},{35,3},{4,36},{36... | collective-permute-start | bytes 1228808 | tf_op jit(solution)/shard_map/ppermute | solution.py:339
  67.8 8.9 %collective-permute-start.12 = (bf16[200,8,128]{2,1,0:T(8,128)(2,1)S(1)}, bf16[200,8,128]{2,1,0:T(8,128)(2,1)S(1)}, u32[]{:S(2)}, u32[]{:S(2)}) collective-permute-start(bf16[200,8,128]{2,1,0:T(8,128)(2,1)S(1)} %collective-permute-done.11.refs_2_), channel_id=1, source_target_pairs={{0,32},{32,0},{1,33},{33,1},{2,34},{34,2},{3,35},{35,3},{4,36},{36... | collective-permute-start | bytes 1228808 | tf_op jit(solution)/shard_map/ppermute | solution.py:339
  71.2 7.8 %collective-permute-start.10 = (bf16[200,8,128]{2,1,0:T(8,128)(2,1)S(1)}, bf16[200,8,128]{2,1,0:T(8,128)(2,1)S(1)}, u32[]{:S(2)}, u32[]{:S(2)}) collective-permute-start(bf16[200,8,128]{2,1,0:T(8,128)(2,1)S(1)} %collective-permute-done.9.refs_1_), channel_id=1, source_target_pairs={{0,32},{32,0},{1,33},{33,1},{2,34},{34,2},{3,35},{35,3},{4,36},{36... | collective-permute-start | bytes 1228808 | tf_op jit(solution)/shard_map/ppermute | solution.py:339
  75.4 4.8 %collective-permute-start.8 = (bf16[200,8,128]{2,1,0:T(8,128)(2,1)S(1)}, bf16[200,8,128]{2,1,0:T(8,128)(2,1)S(1)}, u32[]{:S(2)}, u32[]{:S(2)}) collective-permute-start(bf16[200,8,128]{2,1,0:T(8,128)(2,1)S(1)} %collective-permute-done.7.refs_3_), channel_id=1, source_target_pairs={{0,32},{32,0},{1,33},{33,1},{2,34},{34,2},{3,35},{35,3},{4,36},{36... | collective-permute-start | bytes 1228808 | tf_op jit(solution)/shard_map/ppermute | solution.py:339

commit v4 on v3

--- a/solution.py
+++ b/solution.py
@@ -26,13 +26,12 @@
 WSTEPS = 5
 MIB = 1 << 20
 GRANT = 34
-ORDER = (2, 1, 3, 0)
+ORDER = (1, 3, 2, 0)
 WRITES = {
     "write_0": ((0, True), (0, False)),
     "write_1": ((1, True), (1, False)),
-    "write_2": ((3, True),),
-    "write_3": ((3, False), (2, True)),
-    "write_4": ((2, False),),
+    "write_2": ((3, True), (2, True)),
+    "write_3": ((3, False), (2, False)),
 }
 
 
@@ -54,7 +53,7 @@
     pairs = []
     for core in range(2):
         for lead in range(4):
-            pairs += list(zip(line(core, (lead + k) % 4), line(core, lead)))
+            pairs += list(zip(line(core, lead ^ k), line(core, lead)))
     return pairs
 
 
@@ -200,7 +199,7 @@
 
 def pick_kernel(core, lead, v, *outs):
     for k, out in enumerate(outs):
-        start = piece_start(core[0], (lead[0] + k) % 4)
+        start = piece_start(core[0], lead[0] ^ k)
         out[...] = v[pl.ds(pl.multiple_of(start, 32), QUARTER), :].astype(out.dtype)
 
 
@@ -218,7 +217,7 @@
 
 
 def pair_kernel(k, core, lead, v, got, out):
-    start = piece_start(core[0], (lead[0] + k) % 4)
+    start = piece_start(core[0], lead[0] ^ k)
     kept = v[pl.ds(pl.multiple_of(start, 32), QUARTER), :]
     out[...] = (kept + got[...].astype(jnp.float32)).astype(out.dtype)
 
@@ -376,9 +375,9 @@
     out = None
     for parts in WRITES.values():
         indices = [
-            one(piece_index(core, (lead + k) % 4))
+            one(piece_index(core, lead ^ k))
             if own
-            else one(piece_index(1 - core, (other_lead + k) % 4))
+            else one(piece_index(1 - core, other_lead ^ k))
             for k, own in parts
         ]
         parts = [pieces[k] if own else theirs[k] for k, own in parts]

time: 81.5 us -> 83 us (1.018)
  starting transfers between devices: 21.2 us -> 26.1 us
  waiting for transfers between devices: 14.8 us -> 11.9 us
    ppermute x8, starting transfers between devices: 11.1 us -> 17.7 us  [swap_cores(): return lax.ppermute(value, 'c', [(0, 1), (1, 0)])]
    ppermute x3, waiting for transfers between devices: 6.7 us -> 1.35 us  [on_device(): pieces[k] = lax.ppermute(pieces[0], AXES, from_ahead(k))]
    ppermute x3, waiting for transfers between devices: 7.29 us -> 9.76 us  [on_device(): piece = lax.ppermute(piece, AXES, to_ahead(k))]
    ppermute x3, starting transfers between devices: 5.92 us -> 4.29 us  [on_device(): piece = lax.ppermute(piece, AXES, to_ahead(k))]
    pallas_call x5 -> x4, Pallas kernels: 5.64 us -> 5.02 us  [widen(): pl.pallas_call(functools.partial(widen_kernel, count), out_shape=pltpu.HB...]
  transfers between devices with their start and end apart: 14 -> 14, of which waited for: 6 -> 4; matrix products, arithmetic and copies ran while one was open for 0% -> 0% of each run, Pallas kernels for 6% -> 5%
where the time goes in v4:
time: 83 us; the launch traced here: 82.9 us
  blocking collectives  27.3 us (33%)
  starting transfers between devices  26.1 us (31%)
  Pallas kernels  17.2 us (21%)
  waiting for transfers between devices  11.9 us (14%)
    ppermute x8, starting transfers between devices, swap_cores(): return lax.ppermute(value, 'c', [(0, 1), (1, 0)])  17.7 us
    all_to_all x1, blocking collectives, on_device(): lax.all_to_all(parts, AXES, 0, 0, axis_index_groups=SIXTEENS, tiled=True)  16.1 us
    pallas_call x1, Pallas kernels, gradient(): pl.pallas_call(gradient_kernel, out_shape=pltpu.VMEM((D, D), jnp.float32)...  11.3 us
    all_to_all x1, blocking collectives, on_device(): lax.all_to_all(update, AXES, 0, 0, axis_index_groups=SIXTEENS, tiled=True)  11.3 us
    ppermute x3, waiting for transfers between devices, on_device(): piece = lax.ppermute(piece, AXES, to_ahead(k))  9.76 us
    pallas_call x4, Pallas kernels, widen(): pl.pallas_call(functools.partial(widen_kernel, count), out_shape=pltpu.HB...  5.02 us
    ppermute x3, starting transfers between devices, on_device(): piece = lax.ppermute(piece, AXES, to_ahead(k))  4.29 us
    ppermute x3, starting transfers between devices, on_device(): pieces[k] = lax.ppermute(pieces[0], AXES, from_ahead(k))  4.11 us
  transfers between devices with their start and end apart: 14, of which 4 were waited for; matrix products, arithmetic and copies ran while one was open for 0% of the time, Pallas kernels for 5%

profile of v4, /device:TPU:1, one launch (start us, length us, event | category | flops | bytes accessed | tf_op | source)
XLA Modules:
  0.0 82.9 jit_solution(10468120762649365465)
XLA Ops:
  0.0 11.3 %gradient.1.v = f32[1280,1280]{1,0:T(8,128)S(1)} custom-call(s32[1]{0:T(128)} %bitcast.4.spot, bf16[2048,1280]{1,0:T(8,128)(2,1)} %act.1, bf16[2048,1280]{1,0:T(8,128)(2,1)} %cot.1, f32[1280,1280]{1,0:T(8,128)} %bitcast.18, f32[10,1280]{1,0:T(8,128)} %owner.2), custom_call_target="tpu_custom_call" | custom-call | flops 6710886400 | bytes 17825792 | tf_op jit(solution)/shard_map/gradient/pallas_call | solution.py:170
  11.3 0.2 pick.1
  11.5 1.5 %collective-permute-start.5 = (bf16[160,1280]{1,0:T(8,128)(2,1)S(1)}, bf16[160,1280]{1,0:T(8,128)(2,1)S(1)}, u32[]{:S(2)}, u32[]{:S(2)}) collective-permute-start(bf16[160,1280]{1,0:T(8,128)(2,1)S(1)} %get-tuple-element.12), channel_id=1, source_target_pairs={{0,32},{32,0},{1,33},{33,1},{2,34},{34,2},{3,35},{35,3},{4,36},{36... | collective-permute-start | bytes 1228808 | tf_op jit(solution)/shard_map/ppermute | solution.py:338
  13.0 0.1 collective-permute-start.3
  13.1 0.4 collective-permute-start.1
  13.5 0.1 collective-permute-start
  13.6 0.8 collective-permute-done.5.got
  14.4 0.1 shard_map.49
  14.5 1.5 %collective-permute-start.6 = (bf16[160,1280]{1,0:T(8,128)(2,1)S(1)}, bf16[160,1280]{1,0:T(8,128)(2,1)S(1)}, u32[]{:S(2)}, u32[]{:S(2)}) collective-permute-start(bf16[160,1280]{1,0:T(8,128)(2,1)S(1)} %shard_map.49), channel_id=1, source_target_pairs={{0,1},{4,5},{8,9},{12,13},{16,17},{20,21},{24,25},{28,29},{64,65},... | collective-permute-start | bytes 1228808 | tf_op jit(solution)/shard_map/ppermute | solution.py:363
  15.9 0.0 collective-permute-done.3.got
  15.9 0.1 shard_map.48
  16.0 2.0 %collective-permute-start.4 = (bf16[160,1280]{1,0:T(8,128)(2,1)S(1)}, bf16[160,1280]{1,0:T(8,128)(2,1)S(1)}, u32[]{:S(2)}, u32[]{:S(2)}) collective-permute-start(bf16[160,1280]{1,0:T(8,128)(2,1)S(1)} %shard_map.48), channel_id=1, source_target_pairs={{0,3},{4,7},{8,11},{12,15},{16,19},{20,23},{24,27},{28,31},{64,67}... | collective-permute-start | bytes 1228808 | tf_op jit(solution)/shard_map/ppermute | solution.py:363
  18.0 0.0 collective-permute-done.1.got
  18.0 0.1 shard_map.47
  18.1 0.8 collective-permute-start.2
  19.0 0.0 collective-permute-done.got
  19.0 0.1 shard_map.46.own
  19.1 2.6 %collective-permute-done.6.rest_2_ = bf16[160,1280]{1,0:T(8,128)(2,1)S(1)} collective-permute-done((bf16[160,1280]{1,0:T(8,128)(2,1)S(1)}, bf16[160,1280]{1,0:T(8,128)(2,1)S(1)}, u32[]{:S(2)}, u32[]{:S(2)}) %collective-permute-start.6) | collective-permute-done | bytes 409632 | tf_op jit(solution)/shard_map/ppermute | solution.py:363
  21.6 7.2 %collective-permute-done.4.rest_1_ = bf16[160,1280]{1,0:T(8,128)(2,1)S(1)} collective-permute-done((bf16[160,1280]{1,0:T(8,128)(2,1)S(1)}, bf16[160,1280]{1,0:T(8,128)(2,1)S(1)}, u32[]{:S(2)}, u32[]{:S(2)}) %collective-permute-start.4) | collective-permute-done | bytes 409632 | tf_op jit(solution)/shard_map/ppermute | solution.py:363
  28.8 0.0 collective-permute-done.2.rest_0_
  28.8 0.2 total.1
  29.0 16.1 %all_to_all.10.parts = bf16[16,104,128]{2,1,0:T(8,128)(2,1)S(1)} all-to-all(bf16[16,104,128]{2,1,0:T(8,128)(2,1)S(1)} %bitcast.16), channel_id=1, replica_groups={{0,4,8,12,16,20,24,28,64,68,72,76,80,84,88,92},{1,5,9,13,17,21,25,29,65..., dimensions={0} | all-to-all | bytes 851968 | tf_op jit(solution)/shard_map/all_to_all | solution.py:366
  45.1 0.2 owner.3
  45.2 11.3 %all_to_all.11 = bf16[16,104,128]{2,1,0:T(8,128)(2,1)S(1)} all-to-all(bf16[16,104,128]{2,1,0:T(8,128)(2,1)S(1)} %owner.3), channel_id=1, replica_groups={{0,4,8,12,16,20,24,28,64,68,72,76,80,84,88,92},{1,5,9,13,17,21,25,29,65..., dimensions={0} | all-to-all | bytes 851968 | tf_op jit(solution)/shard_map/all_to_all | solution.py:368
  56.5 0.3 collective-permute-start.11
  56.8 3.0 %collective-permute-start.9 = (bf16[200,8,128]{2,1,0:T(8,128)(2,1)S(1)}, bf16[200,8,128]{2,1,0:T(8,128)(2,1)S(1)}, u32[]{:S(2)}, u32[]{:S(2)}) collective-permute-start(bf16[200,8,128]{2,1,0:T(8,128)(2,1)S(1)} %slice.4.refs_2_), channel_id=1, source_target_pairs={{2,0},{6,4},{10,8},{14,12},{18,16},{22,20},{26,24},{30,28},{66,64}... | collective-permute-start | bytes 1228808 | tf_op jit(solution)/shard_map/ppermute | solution.py:371
  59.8 0.8 collective-permute-start.7
  60.7 4.7 %collective-permute-start.13 = (bf16[200,8,128]{2,1,0:T(8,128)(2,1)S(1)}, bf16[200,8,128]{2,1,0:T(8,128)(2,1)S(1)}, u32[]{:S(2)}, u32[]{:S(2)}) collective-permute-start(bf16[200,8,128]{2,1,0:T(8,128)(2,1)S(1)} %slice.4.refs_2_), channel_id=1, source_target_pairs={{0,32},{32,0},{1,33},{33,1},{2,34},{34,2},{3,35},{35,3},{4,36},{36... | collective-permute-start | bytes 1228808 | tf_op jit(solution)/shard_map/ppermute | solution.py:338
  65.3 0.0 collective-permute-done.11.refs_2_
  65.3 3.2 %collective-permute-start.12 = (bf16[200,8,128]{2,1,0:T(8,128)(2,1)S(1)}, bf16[200,8,128]{2,1,0:T(8,128)(2,1)S(1)}, u32[]{:S(2)}, u32[]{:S(2)}) collective-permute-start(bf16[200,8,128]{2,1,0:T(8,128)(2,1)S(1)} %collective-permute-done.11.refs_2_), channel_id=1, source_target_pairs={{0,32},{32,0},{1,33},{33,1},{2,34},{34,2},{3,35},{35,3},{4,36},{36... | collective-permute-start | bytes 1228808 | tf_op jit(solution)/shard_map/ppermute | solution.py:338
  68.6 1.3 %collective-permute-done.9.refs_3_ = bf16[200,8,128]{2,1,0:T(8,128)(2,1)S(1)} collective-permute-done((bf16[200,8,128]{2,1,0:T(8,128)(2,1)S(1)}, bf16[200,8,128]{2,1,0:T(8,128)(2,1)S(1)}, u32[]{:S(2)}, u32[]{:S(2)}) %collective-permute-start.9) | collective-permute-done | bytes 409632 | tf_op jit(solution)/shard_map/ppermute | solution.py:371
  69.9 4.6 %collective-permute-start.10 = (bf16[200,8,128]{2,1,0:T(8,128)(2,1)S(1)}, bf16[200,8,128]{2,1,0:T(8,128)(2,1)S(1)}, u32[]{:S(2)}, u32[]{:S(2)}) collective-permute-start(bf16[200,8,128]{2,1,0:T(8,128)(2,1)S(1)} %collective-permute-done.9.refs_3_), channel_id=1, source_target_pairs={{0,32},{32,0},{1,33},{33,1},{2,34},{34,2},{3,35},{35,3},{4,36},{36... | collective-permute-start | bytes 1228808 | tf_op jit(solution)/shard_map/ppermute | solution.py:338
  74.5 0.0 collective-permute-done.7.refs_2_
  74.5 3.1 %collective-permute-start.8 = (bf16[200,8,128]{2,1,0:T(8,128)(2,1)S(1)}, bf16[200,8,128]{2,1,0:T(8,128)(2,1)S(1)}, u32[]{:S(2)}, u32[]{:S(2)}) collective-permute-start(bf16[200,8,128]{2,1,0:T(8,128)(2,1)S(1)} %collective-permute-done.7.refs_2_), channel_id=1, source_target_pairs={{0,32},{32,0},{1,33},{33,1},{2,34},{34,2},{3,35},{35,3},{4,36},{36... | collective-permute-start | bytes 1228808 | tf_op jit(solution)/shard_map/ppermute | solution.py:338
  77.6 0.0 collective-permute-done.13.refs_3_
  77.6 1.2 %widen.4.refs_4_ = f32[1280,1280]{1,0:T(8,128)} custom-call(s32[1]{0:T(128)} %bitcast.14.refs_0_, s32[1]{0:T(128)} %bitcast.15.refs_1_, bf16[200,8,128]{2,1,0:T(8,128)(2,1)S(1)} %slice.4.refs_2_, bf16[200,8,128]{2,1,0:T(8,128)(2,1)S(1)} %collective-permute-done.13.refs_3_), custom_call_target="tpu_custom_call" | custom-call | flops 1073741824 | bytes 1048576 | tf_op jit(solution)/shard_map/widen/pallas_call | solution.py:321
  78.9 0.0 collective-permute-done.12.refs_3_
  78.9 1.3 %widen.5.refs_4_ = f32[1280,1280]{1,0:T(8,128)} custom-call(s32[1]{0:T(128)} %bitcast.12.refs_0_, s32[1]{0:T(128)} %bitcast.13.refs_1_, bf16[200,8,128]{2,1,0:T(8,128)(2,1)S(1)} %collective-permute-done.11.refs_2_, bf16[200,8,128]{2,1,0:T(8,128)(2,1)S(1)} %collective-permute-done.12.refs_3_, f32[1280,1280]{1,0:T(8,128)} %widen.4.refs_4_), custom_call_target="tpu_custom_call", output_to_operand_aliasing={{}: (4, {})} | custom-call | flops 1073741824 | bytes 1048576 | tf_op jit(solution)/shard_map/widen/pallas_call | solution.py:321
  80.2 1.3 %widen.6.refs_4_ = f32[1280,1280]{1,0:T(8,128)} custom-call(s32[1]{0:T(128)} %bitcast.10.refs_0_, s32[1]{0:T(128)} %bitcast.11.refs_1_, bf16[200,8,128]{2,1,0:T(8,128)(2,1)S(1)} %collective-permute-done.7.refs_2_, bf16[200,8,128]{2,1,0:T(8,128)(2,1)S(1)} %collective-permute-done.9.refs_3_, f32[1280,1280]{1,0:T(8,128)} %widen.5.refs_4_), custom_call_target="tpu_custom_call", output_to_operand_aliasing={{}: (4, {})} | custom-call | flops 1073741824 | bytes 1048576 | tf_op jit(solution)/shard_map/widen/pallas_call | solution.py:321
  81.4 0.0 collective-permute-done.10.refs_3_
  81.4 0.0 collective-permute-done.8.refs_2_
  81.5 1.3 %widen.7 = f32[1280,1280]{1,0:T(8,128)} custom-call(s32[1]{0:T(128)} %bitcast.refs_0_, s32[1]{0:T(128)} %bitcast.1.refs_1_, bf16[200,8,128]{2,1,0:T(8,128)(2,1)S(1)} %collective-permute-done.8.refs_2_, bf16[200,8,128]{2,1,0:T(8,128)(2,1)S(1)} %collective-permute-done.10.refs_3_, f32[1280,1280]{1,0:T(8,128)} %widen.6.refs_4_), custom_call_target="tpu_custom_call", output_to_operand_aliasing={{}: (4, {})} | custom-call | flops 1073741824 | bytes 1048576 | tf_op jit(solution)/shard_map/widen/pallas_call | solution.py:321
  (1 shorter events, 0.0 us)
Async XLA Ops:
  11.5 2.8 %collective-permute-start.5 = (bf16[160,1280]{1,0:T(8,128)(2,1)S(1)}, bf16[160,1280]{1,0:T(8,128)(2,1)S(1)}, u32[]{:S(2)}, u32[]{:S(2)}) collective-permute-start(bf16[160,1280]{1,0:T(8,128)(2,1)S(1)} %get-tuple-element.12), channel_id=1, source_target_pairs={{0,32},{32,0},{1,33},{33,1},{2,34},{34,2},{3,35},{35,3},{4,36},{36... | collective-permute-start | bytes 1228808 | tf_op jit(solution)/shard_map/ppermute | solution.py:338
  13.0 2.9 %collective-permute-start.3 = (bf16[160,1280]{1,0:T(8,128)(2,1)S(1)}, bf16[160,1280]{1,0:T(8,128)(2,1)S(1)}, u32[]{:S(2)}, u32[]{:S(2)}) collective-permute-start(bf16[160,1280]{1,0:T(8,128)(2,1)S(1)} %get-tuple-element.11), channel_id=1, source_target_pairs={{0,32},{32,0},{1,33},{33,1},{2,34},{34,2},{3,35},{35,3},{4,36},{36... | collective-permute-start | bytes 1228808 | tf_op jit(solution)/shard_map/ppermute | solution.py:338
  13.1 5.0 %collective-permute-start.1 = (bf16[160,1280]{1,0:T(8,128)(2,1)S(1)}, bf16[160,1280]{1,0:T(8,128)(2,1)S(1)}, u32[]{:S(2)}, u32[]{:S(2)}) collective-permute-start(bf16[160,1280]{1,0:T(8,128)(2,1)S(1)} %get-tuple-element.10), channel_id=1, source_target_pairs={{0,32},{32,0},{1,33},{33,1},{2,34},{34,2},{3,35},{35,3},{4,36},{36... | collective-permute-start | bytes 1228808 | tf_op jit(solution)/shard_map/ppermute | solution.py:338
  13.5 5.5 %collective-permute-start = (bf16[160,1280]{1,0:T(8,128)(2,1)S(1)}, bf16[160,1280]{1,0:T(8,128)(2,1)S(1)}, u32[]{:S(2)}, u32[]{:S(2)}) collective-permute-start(bf16[160,1280]{1,0:T(8,128)(2,1)S(1)} %get-tuple-element.9), channel_id=1, source_target_pairs={{0,32},{32,0},{1,33},{33,1},{2,34},{34,2},{3,35},{35,3},{4,36},{36... | collective-permute-start | bytes 1228808 | tf_op jit(solution)/shard_map/ppermute | solution.py:338
  14.5 7.2 %collective-permute-start.6 = (bf16[160,1280]{1,0:T(8,128)(2,1)S(1)}, bf16[160,1280]{1,0:T(8,128)(2,1)S(1)}, u32[]{:S(2)}, u32[]{:S(2)}) collective-permute-start(bf16[160,1280]{1,0:T(8,128)(2,1)S(1)} %shard_map.49), channel_id=1, source_target_pairs={{0,1},{4,5},{8,9},{12,13},{16,17},{20,21},{24,25},{28,29},{64,65},... | collective-permute-start | bytes 1228808 | tf_op jit(solution)/shard_map/ppermute | solution.py:363
  16.0 12.8 %collective-permute-start.4 = (bf16[160,1280]{1,0:T(8,128)(2,1)S(1)}, bf16[160,1280]{1,0:T(8,128)(2,1)S(1)}, u32[]{:S(2)}, u32[]{:S(2)}) collective-permute-start(bf16[160,1280]{1,0:T(8,128)(2,1)S(1)} %shard_map.48), channel_id=1, source_target_pairs={{0,3},{4,7},{8,11},{12,15},{16,19},{20,23},{24,27},{28,31},{64,67}... | collective-permute-start | bytes 1228808 | tf_op jit(solution)/shard_map/ppermute | solution.py:363
  18.1 10.7 %collective-permute-start.2 = (bf16[160,1280]{1,0:T(8,128)(2,1)S(1)}, bf16[160,1280]{1,0:T(8,128)(2,1)S(1)}, u32[]{:S(2)}, u32[]{:S(2)}) collective-permute-start(bf16[160,1280]{1,0:T(8,128)(2,1)S(1)} %shard_map.47), channel_id=1, source_target_pairs={{0,2},{4,6},{8,10},{12,14},{16,18},{20,22},{24,26},{28,30},{64,66}... | collective-permute-start | bytes 1228808 | tf_op jit(solution)/shard_map/ppermute | solution.py:363
  56.5 8.8 %collective-permute-start.11 = (bf16[200,8,128]{2,1,0:T(8,128)(2,1)S(1)}, bf16[200,8,128]{2,1,0:T(8,128)(2,1)S(1)}, u32[]{:S(2)}, u32[]{:S(2)}) collective-permute-start(bf16[200,8,128]{2,1,0:T(8,128)(2,1)S(1)} %slice.4.refs_2_), channel_id=1, source_target_pairs={{1,0},{5,4},{9,8},{13,12},{17,16},{21,20},{25,24},{29,28},{65,64},... | collective-permute-start | bytes 1228808 | tf_op jit(solution)/shard_map/ppermute | solution.py:371
  56.8 13.1 %collective-permute-start.9 = (bf16[200,8,128]{2,1,0:T(8,128)(2,1)S(1)}, bf16[200,8,128]{2,1,0:T(8,128)(2,1)S(1)}, u32[]{:S(2)}, u32[]{:S(2)}) collective-permute-start(bf16[200,8,128]{2,1,0:T(8,128)(2,1)S(1)} %slice.4.refs_2_), channel_id=1, source_target_pairs={{2,0},{6,4},{10,8},{14,12},{18,16},{22,20},{26,24},{30,28},{66,64}... | collective-permute-start | bytes 1228808 | tf_op jit(solution)/shard_map/ppermute | solution.py:371
  59.8 14.7 %collective-permute-start.7 = (bf16[200,8,128]{2,1,0:T(8,128)(2,1)S(1)}, bf16[200,8,128]{2,1,0:T(8,128)(2,1)S(1)}, u32[]{:S(2)}, u32[]{:S(2)}) collective-permute-start(bf16[200,8,128]{2,1,0:T(8,128)(2,1)S(1)} %slice.4.refs_2_), channel_id=1, source_target_pairs={{3,0},{7,4},{11,8},{15,12},{19,16},{23,20},{27,24},{31,28},{67,64}... | collective-permute-start | bytes 1228808 | tf_op jit(solution)/shard_map/ppermute | solution.py:371
  60.7 17.0 %collective-permute-start.13 = (bf16[200,8,128]{2,1,0:T(8,128)(2,1)S(1)}, bf16[200,8,128]{2,1,0:T(8,128)(2,1)S(1)}, u32[]{:S(2)}, u32[]{:S(2)}) collective-permute-start(bf16[200,8,128]{2,1,0:T(8,128)(2,1)S(1)} %slice.4.refs_2_), channel_id=1, source_target_pairs={{0,32},{32,0},{1,33},{33,1},{2,34},{34,2},{3,35},{35,3},{4,36},{36... | collective-permute-start | bytes 1228808 | tf_op jit(solution)/shard_map/ppermute | solution.py:338
  65.3 13.6 %collective-permute-start.12 = (bf16[200,8,128]{2,1,0:T(8,128)(2,1)S(1)}, bf16[200,8,128]{2,1,0:T(8,128)(2,1)S(1)}, u32[]{:S(2)}, u32[]{:S(2)}) collective-permute-start(bf16[200,8,128]{2,1,0:T(8,128)(2,1)S(1)} %collective-permute-done.11.refs_2_), channel_id=1, source_target_pairs={{0,32},{32,0},{1,33},{33,1},{2,34},{34,2},{3,35},{35,3},{4,36},{36... | collective-permute-start | bytes 1228808 | tf_op jit(solution)/shard_map/ppermute | solution.py:338
  69.9 11.5 %collective-permute-start.10 = (bf16[200,8,128]{2,1,0:T(8,128)(2,1)S(1)}, bf16[200,8,128]{2,1,0:T(8,128)(2,1)S(1)}, u32[]{:S(2)}, u32[]{:S(2)}) collective-permute-start(bf16[200,8,128]{2,1,0:T(8,128)(2,1)S(1)} %collective-permute-done.9.refs_3_), channel_id=1, source_target_pairs={{0,32},{32,0},{1,33},{33,1},{2,34},{34,2},{3,35},{35,3},{4,36},{36... | collective-permute-start | bytes 1228808 | tf_op jit(solution)/shard_map/ppermute | solution.py:338
  74.5 6.9 %collective-permute-start.8 = (bf16[200,8,128]{2,1,0:T(8,128)(2,1)S(1)}, bf16[200,8,128]{2,1,0:T(8,128)(2,1)S(1)}, u32[]{:S(2)}, u32[]{:S(2)}) collective-permute-start(bf16[200,8,128]{2,1,0:T(8,128)(2,1)S(1)} %collective-permute-done.7.refs_2_), channel_id=1, source_target_pairs={{0,32},{32,0},{1,33},{33,1},{2,34},{34,2},{3,35},{35,3},{4,36},{36... | collective-permute-start | bytes 1228808 | tf_op jit(solution)/shard_map/ppermute | solution.py:338

commit v5 on v4

--- a/solution.py
+++ b/solution.py
@@ -22,8 +22,9 @@
 OWNED = PER_CHIP * 8
 CHUNK = 512
 MROWS = 256
-EARLY = 3
-WSTEPS = 5
+EARLY = 4
+AHEAD = 3
+WSTEPS = 2
 MIB = 1 << 20
 GRANT = 34
 ORDER = (1, 3, 2, 0)
@@ -117,16 +118,16 @@
             v[at, cols] = quantized(acc[at, cols] + err[at, cols])
 
     load_own = pltpu.make_async_copy(owner, own, own_sem)
-    for i in range(2):
+    for i in range(AHEAD):
         for copy in early(i):
             copy.start()
     for i in range(chunks):
         for copy in early(i):
             copy.wait()
-        if i + 2 < chunks:
-            for copy in early(i + 2):
+        if i + AHEAD < chunks:
+            for copy in early(i + AHEAD):
                 copy.start()
-        elif i + 2 == chunks:
+        elif i + AHEAD == chunks:
             late(EARLY).start()
             for j in range(blocks):
                 load_err(j).start()

time: 83 us -> 82.9 us (level)
  no operation moved by 1% of the time
where the time goes in v5:
time: 82.9 us; the launch traced here: 82.7 us
  blocking collectives  27.4 us (33%)
  starting transfers between devices  25.9 us (31%)
  Pallas kernels  17 us (21%)
  waiting for transfers between devices  12.1 us (15%)
    ppermute x8, starting transfers between devices, swap_cores(): return lax.ppermute(value, 'c', [(0, 1), (1, 0)])  17.7 us
    all_to_all x1, blocking collectives, on_device(): lax.all_to_all(parts, AXES, 0, 0, axis_index_groups=SIXTEENS, tiled=True)  16.1 us
    all_to_all x1, blocking collectives, on_device(): lax.all_to_all(update, AXES, 0, 0, axis_index_groups=SIXTEENS, tiled=True)  11.4 us
    pallas_call x1, Pallas kernels, gradient(): pl.pallas_call(gradient_kernel, out_shape=pltpu.VMEM((D, D), jnp.float32)...  11.2 us
    ppermute x3, waiting for transfers between devices, on_device(): piece = lax.ppermute(piece, AXES, to_ahead(k))  9.78 us
    pallas_call x4, Pallas kernels, widen(): pl.pallas_call(functools.partial(widen_kernel, count), out_shape=pltpu.HB...  4.89 us
    ppermute x3, starting transfers between devices, on_device(): piece = lax.ppermute(piece, AXES, to_ahead(k))  4.29 us
    ppermute x3, starting transfers between devices, on_device(): pieces[k] = lax.ppermute(pieces[0], AXES, from_ahead(k))  3.93 us
  transfers between devices with their start and end apart: 14, of which 4 were waited for; matrix products, arithmetic and copies ran while one was open for 0% of the time, Pallas kernels for 5%

profile of v5, /device:TPU:1, one launch (start us, length us, event | category | flops | bytes accessed | tf_op | source)
XLA Modules:
  0.0 82.7 jit_solution(16339938968196315960)
XLA Ops:
  0.0 11.2 %gradient.1.v = f32[1280,1280]{1,0:T(8,128)S(1)} custom-call(s32[1]{0:T(128)} %bitcast.4.spot, bf16[2048,1280]{1,0:T(8,128)(2,1)} %act.1, bf16[2048,1280]{1,0:T(8,128)(2,1)} %cot.1, f32[1280,1280]{1,0:T(8,128)} %bitcast.18, f32[10,1280]{1,0:T(8,128)} %owner.2), custom_call_target="tpu_custom_call" | custom-call | flops 6710886400 | bytes 17825792 | tf_op jit(solution)/shard_map/gradient/pallas_call | solution.py:171
  11.2 0.2 pick.1
  11.4 1.5 %collective-permute-start.5 = (bf16[160,1280]{1,0:T(8,128)(2,1)S(1)}, bf16[160,1280]{1,0:T(8,128)(2,1)S(1)}, u32[]{:S(2)}, u32[]{:S(2)}) collective-permute-start(bf16[160,1280]{1,0:T(8,128)(2,1)S(1)} %get-tuple-element.12), channel_id=1, source_target_pairs={{0,32},{32,0},{1,33},{33,1},{2,34},{34,2},{3,35},{35,3},{4,36},{36... | collective-permute-start | bytes 1228808 | tf_op jit(solution)/shard_map/ppermute | solution.py:339
  12.8 0.1 collective-permute-start.3
  12.9 0.4 collective-permute-start.1
  13.3 0.1 collective-permute-start
  13.4 0.8 collective-permute-done.5.got
  14.2 0.1 shard_map.49
  14.3 1.5 %collective-permute-start.6 = (bf16[160,1280]{1,0:T(8,128)(2,1)S(1)}, bf16[160,1280]{1,0:T(8,128)(2,1)S(1)}, u32[]{:S(2)}, u32[]{:S(2)}) collective-permute-start(bf16[160,1280]{1,0:T(8,128)(2,1)S(1)} %shard_map.49), channel_id=1, source_target_pairs={{0,1},{4,5},{8,9},{12,13},{16,17},{20,21},{24,25},{28,29},{64,65},... | collective-permute-start | bytes 1228808 | tf_op jit(solution)/shard_map/ppermute | solution.py:364
  15.8 0.0 collective-permute-done.3.got
  15.8 0.1 shard_map.48
  15.9 2.0 %collective-permute-start.4 = (bf16[160,1280]{1,0:T(8,128)(2,1)S(1)}, bf16[160,1280]{1,0:T(8,128)(2,1)S(1)}, u32[]{:S(2)}, u32[]{:S(2)}) collective-permute-start(bf16[160,1280]{1,0:T(8,128)(2,1)S(1)} %shard_map.48), channel_id=1, source_target_pairs={{0,3},{4,7},{8,11},{12,15},{16,19},{20,23},{24,27},{28,31},{64,67}... | collective-permute-start | bytes 1228808 | tf_op jit(solution)/shard_map/ppermute | solution.py:364
  17.9 0.0 collective-permute-done.1.got
  17.9 0.1 shard_map.47
  18.0 0.8 collective-permute-start.2
  18.8 0.0 collective-permute-done.got
  18.8 0.1 shard_map.46.own
  18.9 2.6 %collective-permute-done.6.rest_2_ = bf16[160,1280]{1,0:T(8,128)(2,1)S(1)} collective-permute-done((bf16[160,1280]{1,0:T(8,128)(2,1)S(1)}, bf16[160,1280]{1,0:T(8,128)(2,1)S(1)}, u32[]{:S(2)}, u32[]{:S(2)}) %collective-permute-start.6) | collective-permute-done | bytes 409632 | tf_op jit(solution)/shard_map/ppermute | solution.py:364
  21.5 7.2 %collective-permute-done.4.rest_1_ = bf16[160,1280]{1,0:T(8,128)(2,1)S(1)} collective-permute-done((bf16[160,1280]{1,0:T(8,128)(2,1)S(1)}, bf16[160,1280]{1,0:T(8,128)(2,1)S(1)}, u32[]{:S(2)}, u32[]{:S(2)}) %collective-permute-start.4) | collective-permute-done | bytes 409632 | tf_op jit(solution)/shard_map/ppermute | solution.py:364
  28.7 0.0 collective-permute-done.2.rest_0_
  28.7 0.2 total.1
  28.9 16.1 %all_to_all.10.parts = bf16[16,104,128]{2,1,0:T(8,128)(2,1)S(1)} all-to-all(bf16[16,104,128]{2,1,0:T(8,128)(2,1)S(1)} %bitcast.16), channel_id=1, replica_groups={{0,4,8,12,16,20,24,28,64,68,72,76,80,84,88,92},{1,5,9,13,17,21,25,29,65..., dimensions={0} | all-to-all | bytes 851968 | tf_op jit(solution)/shard_map/all_to_all | solution.py:367
  44.9 0.2 owner.3
  45.1 11.4 %all_to_all.11 = bf16[16,104,128]{2,1,0:T(8,128)(2,1)S(1)} all-to-all(bf16[16,104,128]{2,1,0:T(8,128)(2,1)S(1)} %owner.3), channel_id=1, replica_groups={{0,4,8,12,16,20,24,28,64,68,72,76,80,84,88,92},{1,5,9,13,17,21,25,29,65..., dimensions={0} | all-to-all | bytes 851968 | tf_op jit(solution)/shard_map/all_to_all | solution.py:369
  56.5 0.1 collective-permute-start.11
  56.6 3.2 %collective-permute-start.9 = (bf16[200,8,128]{2,1,0:T(8,128)(2,1)S(1)}, bf16[200,8,128]{2,1,0:T(8,128)(2,1)S(1)}, u32[]{:S(2)}, u32[]{:S(2)}) collective-permute-start(bf16[200,8,128]{2,1,0:T(8,128)(2,1)S(1)} %slice.4.refs_2_), channel_id=1, source_target_pairs={{2,0},{6,4},{10,8},{14,12},{18,16},{22,20},{26,24},{30,28},{66,64}... | collective-permute-start | bytes 1228808 | tf_op jit(solution)/shard_map/ppermute | solution.py:372
  59.7 0.7 collective-permute-start.7
  60.4 4.6 %collective-permute-start.13 = (bf16[200,8,128]{2,1,0:T(8,128)(2,1)S(1)}, bf16[200,8,128]{2,1,0:T(8,128)(2,1)S(1)}, u32[]{:S(2)}, u32[]{:S(2)}) collective-permute-start(bf16[200,8,128]{2,1,0:T(8,128)(2,1)S(1)} %slice.4.refs_2_), channel_id=1, source_target_pairs={{0,32},{32,0},{1,33},{33,1},{2,34},{34,2},{3,35},{35,3},{4,36},{36... | collective-permute-start | bytes 1228808 | tf_op jit(solution)/shard_map/ppermute | solution.py:339
  65.0 0.0 collective-permute-done.11.refs_2_
  65.0 3.2 %collective-permute-start.12 = (bf16[200,8,128]{2,1,0:T(8,128)(2,1)S(1)}, bf16[200,8,128]{2,1,0:T(8,128)(2,1)S(1)}, u32[]{:S(2)}, u32[]{:S(2)}) collective-permute-start(bf16[200,8,128]{2,1,0:T(8,128)(2,1)S(1)} %collective-permute-done.11.refs_2_), channel_id=1, source_target_pairs={{0,32},{32,0},{1,33},{33,1},{2,34},{34,2},{3,35},{35,3},{4,36},{36... | collective-permute-start | bytes 1228808 | tf_op jit(solution)/shard_map/ppermute | solution.py:339
  68.3 1.5 %collective-permute-done.9.refs_3_ = bf16[200,8,128]{2,1,0:T(8,128)(2,1)S(1)} collective-permute-done((bf16[200,8,128]{2,1,0:T(8,128)(2,1)S(1)}, bf16[200,8,128]{2,1,0:T(8,128)(2,1)S(1)}, u32[]{:S(2)}, u32[]{:S(2)}) %collective-permute-start.9) | collective-permute-done | bytes 409632 | tf_op jit(solution)/shard_map/ppermute | solution.py:372
  69.8 4.6 %collective-permute-start.10 = (bf16[200,8,128]{2,1,0:T(8,128)(2,1)S(1)}, bf16[200,8,128]{2,1,0:T(8,128)(2,1)S(1)}, u32[]{:S(2)}, u32[]{:S(2)}) collective-permute-start(bf16[200,8,128]{2,1,0:T(8,128)(2,1)S(1)} %collective-permute-done.9.refs_3_), channel_id=1, source_target_pairs={{0,32},{32,0},{1,33},{33,1},{2,34},{34,2},{3,35},{35,3},{4,36},{36... | collective-permute-start | bytes 1228808 | tf_op jit(solution)/shard_map/ppermute | solution.py:339
  74.4 0.0 collective-permute-done.7.refs_2_
  74.4 3.1 %collective-permute-start.8 = (bf16[200,8,128]{2,1,0:T(8,128)(2,1)S(1)}, bf16[200,8,128]{2,1,0:T(8,128)(2,1)S(1)}, u32[]{:S(2)}, u32[]{:S(2)}) collective-permute-start(bf16[200,8,128]{2,1,0:T(8,128)(2,1)S(1)} %collective-permute-done.7.refs_2_), channel_id=1, source_target_pairs={{0,32},{32,0},{1,33},{33,1},{2,34},{34,2},{3,35},{35,3},{4,36},{36... | collective-permute-start | bytes 1228808 | tf_op jit(solution)/shard_map/ppermute | solution.py:339
  77.6 0.0 collective-permute-done.13.refs_3_
  77.6 1.2 %widen.4.refs_4_ = f32[1280,1280]{1,0:T(8,128)} custom-call(s32[1]{0:T(128)} %bitcast.14.refs_0_, s32[1]{0:T(128)} %bitcast.15.refs_1_, bf16[200,8,128]{2,1,0:T(8,128)(2,1)S(1)} %slice.4.refs_2_, bf16[200,8,128]{2,1,0:T(8,128)(2,1)S(1)} %collective-permute-done.13.refs_3_), custom_call_target="tpu_custom_call" | custom-call | flops 1073741824 | bytes 1048576 | tf_op jit(solution)/shard_map/widen/pallas_call | solution.py:322
  78.8 0.0 collective-permute-done.12.refs_3_
  78.8 1.2 %widen.5.refs_4_ = f32[1280,1280]{1,0:T(8,128)} custom-call(s32[1]{0:T(128)} %bitcast.12.refs_0_, s32[1]{0:T(128)} %bitcast.13.refs_1_, bf16[200,8,128]{2,1,0:T(8,128)(2,1)S(1)} %collective-permute-done.11.refs_2_, bf16[200,8,128]{2,1,0:T(8,128)(2,1)S(1)} %collective-permute-done.12.refs_3_, f32[1280,1280]{1,0:T(8,128)} %widen.4.refs_4_), custom_call_target="tpu_custom_call", output_to_operand_aliasing={{}: (4, {})} | custom-call | flops 1073741824 | bytes 1048576 | tf_op jit(solution)/shard_map/widen/pallas_call | solution.py:322
  80.0 1.2 %widen.6.refs_4_ = f32[1280,1280]{1,0:T(8,128)} custom-call(s32[1]{0:T(128)} %bitcast.10.refs_0_, s32[1]{0:T(128)} %bitcast.11.refs_1_, bf16[200,8,128]{2,1,0:T(8,128)(2,1)S(1)} %collective-permute-done.7.refs_2_, bf16[200,8,128]{2,1,0:T(8,128)(2,1)S(1)} %collective-permute-done.9.refs_3_, f32[1280,1280]{1,0:T(8,128)} %widen.5.refs_4_), custom_call_target="tpu_custom_call", output_to_operand_aliasing={{}: (4, {})} | custom-call | flops 1073741824 | bytes 1048576 | tf_op jit(solution)/shard_map/widen/pallas_call | solution.py:322
  81.3 0.0 collective-permute-done.10.refs_3_
  81.3 0.0 collective-permute-done.8.refs_2_
  81.3 1.2 %widen.7 = f32[1280,1280]{1,0:T(8,128)} custom-call(s32[1]{0:T(128)} %bitcast.refs_0_, s32[1]{0:T(128)} %bitcast.1.refs_1_, bf16[200,8,128]{2,1,0:T(8,128)(2,1)S(1)} %collective-permute-done.8.refs_2_, bf16[200,8,128]{2,1,0:T(8,128)(2,1)S(1)} %collective-permute-done.10.refs_3_, f32[1280,1280]{1,0:T(8,128)} %widen.6.refs_4_), custom_call_target="tpu_custom_call", output_to_operand_aliasing={{}: (4, {})} | custom-call | flops 1073741824 | bytes 1048576 | tf_op jit(solution)/shard_map/widen/pallas_call | solution.py:322
  (1 shorter events, 0.0 us)
Async XLA Ops:
  11.4 2.8 %collective-permute-start.5 = (bf16[160,1280]{1,0:T(8,128)(2,1)S(1)}, bf16[160,1280]{1,0:T(8,128)(2,1)S(1)}, u32[]{:S(2)}, u32[]{:S(2)}) collective-permute-start(bf16[160,1280]{1,0:T(8,128)(2,1)S(1)} %get-tuple-element.12), channel_id=1, source_target_pairs={{0,32},{32,0},{1,33},{33,1},{2,34},{34,2},{3,35},{35,3},{4,36},{36... | collective-permute-start | bytes 1228808 | tf_op jit(solution)/shard_map/ppermute | solution.py:339
  12.8 3.0 %collective-permute-start.3 = (bf16[160,1280]{1,0:T(8,128)(2,1)S(1)}, bf16[160,1280]{1,0:T(8,128)(2,1)S(1)}, u32[]{:S(2)}, u32[]{:S(2)}) collective-permute-start(bf16[160,1280]{1,0:T(8,128)(2,1)S(1)} %get-tuple-element.11), channel_id=1, source_target_pairs={{0,32},{32,0},{1,33},{33,1},{2,34},{34,2},{3,35},{35,3},{4,36},{36... | collective-permute-start | bytes 1228808 | tf_op jit(solution)/shard_map/ppermute | solution.py:339
  12.9 5.0 %collective-permute-start.1 = (bf16[160,1280]{1,0:T(8,128)(2,1)S(1)}, bf16[160,1280]{1,0:T(8,128)(2,1)S(1)}, u32[]{:S(2)}, u32[]{:S(2)}) collective-permute-start(bf16[160,1280]{1,0:T(8,128)(2,1)S(1)} %get-tuple-element.10), channel_id=1, source_target_pairs={{0,32},{32,0},{1,33},{33,1},{2,34},{34,2},{3,35},{35,3},{4,36},{36... | collective-permute-start | bytes 1228808 | tf_op jit(solution)/shard_map/ppermute | solution.py:339
  13.3 5.5 %collective-permute-start = (bf16[160,1280]{1,0:T(8,128)(2,1)S(1)}, bf16[160,1280]{1,0:T(8,128)(2,1)S(1)}, u32[]{:S(2)}, u32[]{:S(2)}) collective-permute-start(bf16[160,1280]{1,0:T(8,128)(2,1)S(1)} %get-tuple-element.9), channel_id=1, source_target_pairs={{0,32},{32,0},{1,33},{33,1},{2,34},{34,2},{3,35},{35,3},{4,36},{36... | collective-permute-start | bytes 1228808 | tf_op jit(solution)/shard_map/ppermute | solution.py:339
  14.3 7.2 %collective-permute-start.6 = (bf16[160,1280]{1,0:T(8,128)(2,1)S(1)}, bf16[160,1280]{1,0:T(8,128)(2,1)S(1)}, u32[]{:S(2)}, u32[]{:S(2)}) collective-permute-start(bf16[160,1280]{1,0:T(8,128)(2,1)S(1)} %shard_map.49), channel_id=1, source_target_pairs={{0,1},{4,5},{8,9},{12,13},{16,17},{20,21},{24,25},{28,29},{64,65},... | collective-permute-start | bytes 1228808 | tf_op jit(solution)/shard_map/ppermute | solution.py:364
  15.9 12.8 %collective-permute-start.4 = (bf16[160,1280]{1,0:T(8,128)(2,1)S(1)}, bf16[160,1280]{1,0:T(8,128)(2,1)S(1)}, u32[]{:S(2)}, u32[]{:S(2)}) collective-permute-start(bf16[160,1280]{1,0:T(8,128)(2,1)S(1)} %shard_map.48), channel_id=1, source_target_pairs={{0,3},{4,7},{8,11},{12,15},{16,19},{20,23},{24,27},{28,31},{64,67}... | collective-permute-start | bytes 1228808 | tf_op jit(solution)/shard_map/ppermute | solution.py:364
  18.0 10.7 %collective-permute-start.2 = (bf16[160,1280]{1,0:T(8,128)(2,1)S(1)}, bf16[160,1280]{1,0:T(8,128)(2,1)S(1)}, u32[]{:S(2)}, u32[]{:S(2)}) collective-permute-start(bf16[160,1280]{1,0:T(8,128)(2,1)S(1)} %shard_map.47), channel_id=1, source_target_pairs={{0,2},{4,6},{8,10},{12,14},{16,18},{20,22},{24,26},{28,30},{64,66}... | collective-permute-start | bytes 1228808 | tf_op jit(solution)/shard_map/ppermute | solution.py:364
  56.5 8.6 %collective-permute-start.11 = (bf16[200,8,128]{2,1,0:T(8,128)(2,1)S(1)}, bf16[200,8,128]{2,1,0:T(8,128)(2,1)S(1)}, u32[]{:S(2)}, u32[]{:S(2)}) collective-permute-start(bf16[200,8,128]{2,1,0:T(8,128)(2,1)S(1)} %slice.4.refs_2_), channel_id=1, source_target_pairs={{1,0},{5,4},{9,8},{13,12},{17,16},{21,20},{25,24},{29,28},{65,64},... | collective-permute-start | bytes 1228808 | tf_op jit(solution)/shard_map/ppermute | solution.py:372
  56.6 13.2 %collective-permute-start.9 = (bf16[200,8,128]{2,1,0:T(8,128)(2,1)S(1)}, bf16[200,8,128]{2,1,0:T(8,128)(2,1)S(1)}, u32[]{:S(2)}, u32[]{:S(2)}) collective-permute-start(bf16[200,8,128]{2,1,0:T(8,128)(2,1)S(1)} %slice.4.refs_2_), channel_id=1, source_target_pairs={{2,0},{6,4},{10,8},{14,12},{18,16},{22,20},{26,24},{30,28},{66,64}... | collective-permute-start | bytes 1228808 | tf_op jit(solution)/shard_map/ppermute | solution.py:372
  59.7 14.7 %collective-permute-start.7 = (bf16[200,8,128]{2,1,0:T(8,128)(2,1)S(1)}, bf16[200,8,128]{2,1,0:T(8,128)(2,1)S(1)}, u32[]{:S(2)}, u32[]{:S(2)}) collective-permute-start(bf16[200,8,128]{2,1,0:T(8,128)(2,1)S(1)} %slice.4.refs_2_), channel_id=1, source_target_pairs={{3,0},{7,4},{11,8},{15,12},{19,16},{23,20},{27,24},{31,28},{67,64}... | collective-permute-start | bytes 1228808 | tf_op jit(solution)/shard_map/ppermute | solution.py:372
  60.4 17.2 %collective-permute-start.13 = (bf16[200,8,128]{2,1,0:T(8,128)(2,1)S(1)}, bf16[200,8,128]{2,1,0:T(8,128)(2,1)S(1)}, u32[]{:S(2)}, u32[]{:S(2)}) collective-permute-start(bf16[200,8,128]{2,1,0:T(8,128)(2,1)S(1)} %slice.4.refs_2_), channel_id=1, source_target_pairs={{0,32},{32,0},{1,33},{33,1},{2,34},{34,2},{3,35},{35,3},{4,36},{36... | collective-permute-start | bytes 1228808 | tf_op jit(solution)/shard_map/ppermute | solution.py:339
  65.0 13.8 %collective-permute-start.12 = (bf16[200,8,128]{2,1,0:T(8,128)(2,1)S(1)}, bf16[200,8,128]{2,1,0:T(8,128)(2,1)S(1)}, u32[]{:S(2)}, u32[]{:S(2)}) collective-permute-start(bf16[200,8,128]{2,1,0:T(8,128)(2,1)S(1)} %collective-permute-done.11.refs_2_), channel_id=1, source_target_pairs={{0,32},{32,0},{1,33},{33,1},{2,34},{34,2},{3,35},{35,3},{4,36},{36... | collective-permute-start | bytes 1228808 | tf_op jit(solution)/shard_map/ppermute | solution.py:339
  69.8 11.5 %collective-permute-start.10 = (bf16[200,8,128]{2,1,0:T(8,128)(2,1)S(1)}, bf16[200,8,128]{2,1,0:T(8,128)(2,1)S(1)}, u32[]{:S(2)}, u32[]{:S(2)}) collective-permute-start(bf16[200,8,128]{2,1,0:T(8,128)(2,1)S(1)} %collective-permute-done.9.refs_3_), channel_id=1, source_target_pairs={{0,32},{32,0},{1,33},{33,1},{2,34},{34,2},{3,35},{35,3},{4,36},{36... | collective-permute-start | bytes 1228808 | tf_op jit(solution)/shard_map/ppermute | solution.py:339
  74.4 6.9 %collective-permute-start.8 = (bf16[200,8,128]{2,1,0:T(8,128)(2,1)S(1)}, bf16[200,8,128]{2,1,0:T(8,128)(2,1)S(1)}, u32[]{:S(2)}, u32[]{:S(2)}) collective-permute-start(bf16[200,8,128]{2,1,0:T(8,128)(2,1)S(1)} %collective-permute-done.7.refs_2_), channel_id=1, source_target_pairs={{0,32},{32,0},{1,33},{33,1},{2,34},{34,2},{3,35},{35,3},{4,36},{36... | collective-permute-start | bytes 1228808 | tf_op jit(solution)/shard_map/ppermute | solution.py:339

commit v6 on v5

--- a/solution.py
+++ b/solution.py
@@ -86,7 +86,7 @@
 
 
 def gradient_kernel(
-    spot, act, cot, error, owner, v, early_v, late_v, cot_v, err, own, acc, early_sem, late_sem, cot_sem, err_sem, own_sem
+    core, lead, spot, act, cot, error, owner, v, s0, s1, s2, s3, early_v, late_v, cot_v, err, own, acc, early_sem, late_sem, cot_sem, err_sem, own_sem
 ):
     chunks = cot.shape[0] // CHUNK
     blocks = D // MROWS
@@ -162,17 +162,21 @@
                 rows = pl.ds(pl.multiple_of(row // 8 * 8 + 8 * i, 8), 8)
                 mine = own[low - shift + 8 * i : high - shift + 8 * i, :]
                 v[rows, :] = v[rows, :] + jnp.pad(mine, ((low, 8 - high), (0, 0)))
-
-
-def gradient(spot, act, cot, error, owner):
+    for k, out in enumerate((s0, s1, s2, s3)):
+        start = piece_start(core[0], lead[0] ^ k)
+        out[...] = v[pl.ds(pl.multiple_of(start, 32), QUARTER), :].astype(out.dtype)
+
+
+def gradient(core, lead, spot, act, cot, error, owner):
     tokens = act.shape[0]
     hbm, vmem = pl.BlockSpec(memory_space=pltpu.HBM), pl.BlockSpec(memory_space=pltpu.VMEM)
     blocks, chunks = D // MROWS, tokens // CHUNK
     return pl.pallas_call(
         gradient_kernel,
-        out_shape=pltpu.VMEM((D, D), jnp.float32),
-        in_specs=[pl.BlockSpec(memory_space=pltpu.SMEM)] + [hbm] * 4,
-        out_specs=vmem,
+        out_shape=[pltpu.VMEM((D, D), jnp.float32)]
+        + [jax.ShapeDtypeStruct((QUARTER, D), jnp.bfloat16)] * 4,
+        in_specs=[pl.BlockSpec(memory_space=pltpu.SMEM)] * 3 + [hbm] * 4,
+        out_specs=[vmem] * 5,
         scratch_shapes=[
             pltpu.VMEM((tokens, EARLY * MROWS), jnp.bfloat16),
             pltpu.VMEM((blocks - EARLY, tokens, MROWS), jnp.bfloat16),
@@ -191,30 +195,11 @@
             flops=2 * tokens * D * D, bytes_accessed=17 * MIB, transcendentals=0
         ),
         name="gradient",
-    )(spot, act, cot, error, owner)
+    )(core, lead, spot, act, cot, error, owner)
 
 
 def multiplied(a, c):
     return lax.dot_general(a, c, (((0,), (0,)), ((), ())), preferred_element_type=jnp.float32)
-
-
-def pick_kernel(core, lead, v, *outs):
-    for k, out in enumerate(outs):
-        start = piece_start(core[0], lead[0] ^ k)
-        out[...] = v[pl.ds(pl.multiple_of(start, 32), QUARTER), :].astype(out.dtype)
-
-
-def pick(core, lead, v):
-    smem, vmem = pl.BlockSpec(memory_space=pltpu.SMEM), pl.BlockSpec(memory_space=pltpu.VMEM)
-    return pl.pallas_call(
-        pick_kernel,
-        out_shape=[jax.ShapeDtypeStruct((QUARTER, D), jnp.bfloat16)] * 4,
-        in_specs=[smem, smem, vmem],
-        out_specs=[vmem] * 4,
-        compiler_params=params(4),
-        cost_estimate=pl.CostEstimate(flops=1 << 28, bytes_accessed=2 * MIB, transcendentals=0),
-        name="pick",
-    )(core, lead, v)
 
 
 def pair_kernel(k, core, lead, v, got, out):
@@ -352,8 +337,7 @@
     error = carried_error.reshape(D, D)
     args = (activations, cotangent, error, owner_error)
     args = [pltpu.with_memory_space_constraint(v, pltpu.HBM) for v in args]
-    v = gradient(spot, *args)
-    sent = pick(one(1 - core), one(other_lead), v)
+    v, *sent = gradient(one(1 - core), one(other_lead), spot, *args)
     got = {}
     for k in ORDER:
         got[k] = swap_cores(sent[k])

time: 82.9 us -> 82.8 us (level)
    pallas_call x2 -> x1, Pallas kernels: 11.3 us -> 11.3 us  [gradient(): pl.pallas_call(gradient_kernel, out_shape=[pltpu.VMEM((D, D), jnp.float32...]
where the time goes in v6:
time: 82.8 us; the launch traced here: 82.6 us
  blocking collectives  27.4 us (33%)
  starting transfers between devices  25.9 us (31%)
  Pallas kernels  16.9 us (20%)
  waiting for transfers between devices  12.1 us (15%)
    ppermute x8, starting transfers between devices, swap_cores(): return lax.ppermute(value, 'c', [(0, 1), (1, 0)])  17.7 us
    all_to_all x1, blocking collectives, on_device(): lax.all_to_all(parts, AXES, 0, 0, axis_index_groups=SIXTEENS, tiled=True)  16.1 us
    all_to_all x1, blocking collectives, on_device(): lax.all_to_all(update, AXES, 0, 0, axis_index_groups=SIXTEENS, tiled=True)  11.4 us
    pallas_call x1, Pallas kernels, gradient(): pl.pallas_call(gradient_kernel, out_shape=[pltpu.VMEM((D, D), jnp.float32...  11.3 us
    ppermute x3, waiting for transfers between devices, on_device(): piece = lax.ppermute(piece, AXES, to_ahead(k))  9.79 us
    pallas_call x4, Pallas kernels, widen(): pl.pallas_call(functools.partial(widen_kernel, count), out_shape=pltpu.HB...  4.89 us
    ppermute x3, starting transfers between devices, on_device(): piece = lax.ppermute(piece, AXES, to_ahead(k))  4.29 us
    ppermute x3, starting transfers between devices, on_device(): pieces[k] = lax.ppermute(pieces[0], AXES, from_ahead(k))  3.93 us
  transfers between devices with their start and end apart: 14, of which 4 were waited for; matrix products, arithmetic and copies ran while one was open for 0% of the time, Pallas kernels for 5%

profile of v6, /device:TPU:1, one launch (start us, length us, event | category | flops | bytes accessed | tf_op | source)
XLA Modules:
  0.0 82.6 jit_solution(7293071939438883321)
XLA Ops:
  0.0 11.3 %gradient.1 = (f32[1280,1280]{1,0:T(8,128)S(1)}, bf16[160,1280]{1,0:T(8,128)(2,1)S(1)}, bf16[160,1280]{1,0:T(8,128)(2,1)S(1)}, bf16[160,1280]{1,0:T(8,128)(2,1)S(1)}, bf16[160,1280]{1,0:T(8,128)(2,1)S(1)}) custom-call(s32[1]{0:T(128)} %bitcast.4.core, s32[1]{0:T(128)} %bitcast.5.lead, s32[1]{0:T(128)} %bitcast.6.spot, bf16[2048,1280]{1,0:T(8,128)(2,1)} %act.1, ...), custom_call_target="tpu_custom_call" | custom-call | flops 6710886400 | bytes 17825792 | tf_op jit(solution)/shard_map/gradient/pallas_call | solution.py:174
  11.4 1.5 %collective-permute-start.5 = (bf16[160,1280]{1,0:T(8,128)(2,1)S(1)}, bf16[160,1280]{1,0:T(8,128)(2,1)S(1)}, u32[]{:S(2)}, u32[]{:S(2)}) collective-permute-start(bf16[160,1280]{1,0:T(8,128)(2,1)S(1)} %get-tuple-element.14), channel_id=1, source_target_pairs={{0,32},{32,0},{1,33},{33,1},{2,34},{34,2},{3,35},{35,3},{4,36},{36... | collective-permute-start | bytes 1228808 | tf_op jit(solution)/shard_map/ppermute | solution.py:324
  12.8 0.1 collective-permute-start.3
  12.9 0.4 collective-permute-start.1
  13.3 0.1 collective-permute-start
  13.4 0.8 collective-permute-done.5.got
  14.2 0.1 shard_map.49
  14.3 1.5 %collective-permute-start.6 = (bf16[160,1280]{1,0:T(8,128)(2,1)S(1)}, bf16[160,1280]{1,0:T(8,128)(2,1)S(1)}, u32[]{:S(2)}, u32[]{:S(2)}) collective-permute-start(bf16[160,1280]{1,0:T(8,128)(2,1)S(1)} %shard_map.49), channel_id=1, source_target_pairs={{0,1},{4,5},{8,9},{12,13},{16,17},{20,21},{24,25},{28,29},{64,65},... | collective-permute-start | bytes 1228808 | tf_op jit(solution)/shard_map/ppermute | solution.py:348
  15.8 0.0 collective-permute-done.3.got
  15.8 0.1 shard_map.48
  15.8 2.0 %collective-permute-start.4 = (bf16[160,1280]{1,0:T(8,128)(2,1)S(1)}, bf16[160,1280]{1,0:T(8,128)(2,1)S(1)}, u32[]{:S(2)}, u32[]{:S(2)}) collective-permute-start(bf16[160,1280]{1,0:T(8,128)(2,1)S(1)} %shard_map.48), channel_id=1, source_target_pairs={{0,3},{4,7},{8,11},{12,15},{16,19},{20,23},{24,27},{28,31},{64,67}... | collective-permute-start | bytes 1228808 | tf_op jit(solution)/shard_map/ppermute | solution.py:348
  17.8 0.0 collective-permute-done.1.got
  17.8 0.1 shard_map.47
  17.9 0.8 collective-permute-start.2
  18.7 0.0 collective-permute-done.got
  18.7 0.1 shard_map.46.own
  18.8 2.6 %collective-permute-done.6.rest_2_ = bf16[160,1280]{1,0:T(8,128)(2,1)S(1)} collective-permute-done((bf16[160,1280]{1,0:T(8,128)(2,1)S(1)}, bf16[160,1280]{1,0:T(8,128)(2,1)S(1)}, u32[]{:S(2)}, u32[]{:S(2)}) %collective-permute-start.6) | collective-permute-done | bytes 409632 | tf_op jit(solution)/shard_map/ppermute | solution.py:348
  21.4 7.2 %collective-permute-done.4.rest_1_ = bf16[160,1280]{1,0:T(8,128)(2,1)S(1)} collective-permute-done((bf16[160,1280]{1,0:T(8,128)(2,1)S(1)}, bf16[160,1280]{1,0:T(8,128)(2,1)S(1)}, u32[]{:S(2)}, u32[]{:S(2)}) %collective-permute-start.4) | collective-permute-done | bytes 409632 | tf_op jit(solution)/shard_map/ppermute | solution.py:348
  28.6 0.0 collective-permute-done.2.rest_0_
  28.6 0.2 total.1
  28.8 16.1 %all_to_all.10.parts = bf16[16,104,128]{2,1,0:T(8,128)(2,1)S(1)} all-to-all(bf16[16,104,128]{2,1,0:T(8,128)(2,1)S(1)} %bitcast.16), channel_id=1, replica_groups={{0,4,8,12,16,20,24,28,64,68,72,76,80,84,88,92},{1,5,9,13,17,21,25,29,65..., dimensions={0} | all-to-all | bytes 851968 | tf_op jit(solution)/shard_map/all_to_all | solution.py:351
  44.9 0.2 owner.3
  45.0 11.4 %all_to_all.11 = bf16[16,104,128]{2,1,0:T(8,128)(2,1)S(1)} all-to-all(bf16[16,104,128]{2,1,0:T(8,128)(2,1)S(1)} %owner.3), channel_id=1, replica_groups={{0,4,8,12,16,20,24,28,64,68,72,76,80,84,88,92},{1,5,9,13,17,21,25,29,65..., dimensions={0} | all-to-all | bytes 851968 | tf_op jit(solution)/shard_map/all_to_all | solution.py:353
  56.4 0.1 collective-permute-start.11
  56.5 3.2 %collective-permute-start.9 = (bf16[200,8,128]{2,1,0:T(8,128)(2,1)S(1)}, bf16[200,8,128]{2,1,0:T(8,128)(2,1)S(1)}, u32[]{:S(2)}, u32[]{:S(2)}) collective-permute-start(bf16[200,8,128]{2,1,0:T(8,128)(2,1)S(1)} %slice.4.refs_2_), channel_id=1, source_target_pairs={{2,0},{6,4},{10,8},{14,12},{18,16},{22,20},{26,24},{30,28},{66,64}... | collective-permute-start | bytes 1228808 | tf_op jit(solution)/shard_map/ppermute | solution.py:356
  59.7 0.7 collective-permute-start.7
  60.4 4.6 %collective-permute-start.13 = (bf16[200,8,128]{2,1,0:T(8,128)(2,1)S(1)}, bf16[200,8,128]{2,1,0:T(8,128)(2,1)S(1)}, u32[]{:S(2)}, u32[]{:S(2)}) collective-permute-start(bf16[200,8,128]{2,1,0:T(8,128)(2,1)S(1)} %slice.4.refs_2_), channel_id=1, source_target_pairs={{0,32},{32,0},{1,33},{33,1},{2,34},{34,2},{3,35},{35,3},{4,36},{36... | collective-permute-start | bytes 1228808 | tf_op jit(solution)/shard_map/ppermute | solution.py:324
  65.0 0.0 collective-permute-done.11.refs_2_
  65.0 3.2 %collective-permute-start.12 = (bf16[200,8,128]{2,1,0:T(8,128)(2,1)S(1)}, bf16[200,8,128]{2,1,0:T(8,128)(2,1)S(1)}, u32[]{:S(2)}, u32[]{:S(2)}) collective-permute-start(bf16[200,8,128]{2,1,0:T(8,128)(2,1)S(1)} %collective-permute-done.11.refs_2_), channel_id=1, source_target_pairs={{0,32},{32,0},{1,33},{33,1},{2,34},{34,2},{3,35},{35,3},{4,36},{36... | collective-permute-start | bytes 1228808 | tf_op jit(solution)/shard_map/ppermute | solution.py:324
  68.2 1.5 %collective-permute-done.9.refs_3_ = bf16[200,8,128]{2,1,0:T(8,128)(2,1)S(1)} collective-permute-done((bf16[200,8,128]{2,1,0:T(8,128)(2,1)S(1)}, bf16[200,8,128]{2,1,0:T(8,128)(2,1)S(1)}, u32[]{:S(2)}, u32[]{:S(2)}) %collective-permute-start.9) | collective-permute-done | bytes 409632 | tf_op jit(solution)/shard_map/ppermute | solution.py:356
  69.8 4.6 %collective-permute-start.10 = (bf16[200,8,128]{2,1,0:T(8,128)(2,1)S(1)}, bf16[200,8,128]{2,1,0:T(8,128)(2,1)S(1)}, u32[]{:S(2)}, u32[]{:S(2)}) collective-permute-start(bf16[200,8,128]{2,1,0:T(8,128)(2,1)S(1)} %collective-permute-done.9.refs_3_), channel_id=1, source_target_pairs={{0,32},{32,0},{1,33},{33,1},{2,34},{34,2},{3,35},{35,3},{4,36},{36... | collective-permute-start | bytes 1228808 | tf_op jit(solution)/shard_map/ppermute | solution.py:324
  74.4 0.0 collective-permute-done.7.refs_2_
  74.4 3.1 %collective-permute-start.8 = (bf16[200,8,128]{2,1,0:T(8,128)(2,1)S(1)}, bf16[200,8,128]{2,1,0:T(8,128)(2,1)S(1)}, u32[]{:S(2)}, u32[]{:S(2)}) collective-permute-start(bf16[200,8,128]{2,1,0:T(8,128)(2,1)S(1)} %collective-permute-done.7.refs_2_), channel_id=1, source_target_pairs={{0,32},{32,0},{1,33},{33,1},{2,34},{34,2},{3,35},{35,3},{4,36},{36... | collective-permute-start | bytes 1228808 | tf_op jit(solution)/shard_map/ppermute | solution.py:324
  77.5 0.0 collective-permute-done.13.refs_3_
  77.5 1.2 %widen.4.refs_4_ = f32[1280,1280]{1,0:T(8,128)} custom-call(s32[1]{0:T(128)} %bitcast.14.refs_0_, s32[1]{0:T(128)} %bitcast.15.refs_1_, bf16[200,8,128]{2,1,0:T(8,128)(2,1)S(1)} %slice.4.refs_2_, bf16[200,8,128]{2,1,0:T(8,128)(2,1)S(1)} %collective-permute-done.13.refs_3_), custom_call_target="tpu_custom_call" | custom-call | flops 1073741824 | bytes 1048576 | tf_op jit(solution)/shard_map/widen/pallas_call | solution.py:307
  78.8 0.0 collective-permute-done.12.refs_3_
  78.8 1.2 %widen.5.refs_4_ = f32[1280,1280]{1,0:T(8,128)} custom-call(s32[1]{0:T(128)} %bitcast.12.refs_0_, s32[1]{0:T(128)} %bitcast.13.refs_1_, bf16[200,8,128]{2,1,0:T(8,128)(2,1)S(1)} %collective-permute-done.11.refs_2_, bf16[200,8,128]{2,1,0:T(8,128)(2,1)S(1)} %collective-permute-done.12.refs_3_, f32[1280,1280]{1,0:T(8,128)} %widen.4.refs_4_), custom_call_target="tpu_custom_call", output_to_operand_aliasing={{}: (4, {})} | custom-call | flops 1073741824 | bytes 1048576 | tf_op jit(solution)/shard_map/widen/pallas_call | solution.py:307
  80.0 1.2 %widen.6.refs_4_ = f32[1280,1280]{1,0:T(8,128)} custom-call(s32[1]{0:T(128)} %bitcast.10.refs_0_, s32[1]{0:T(128)} %bitcast.11.refs_1_, bf16[200,8,128]{2,1,0:T(8,128)(2,1)S(1)} %collective-permute-done.7.refs_2_, bf16[200,8,128]{2,1,0:T(8,128)(2,1)S(1)} %collective-permute-done.9.refs_3_, f32[1280,1280]{1,0:T(8,128)} %widen.5.refs_4_), custom_call_target="tpu_custom_call", output_to_operand_aliasing={{}: (4, {})} | custom-call | flops 1073741824 | bytes 1048576 | tf_op jit(solution)/shard_map/widen/pallas_call | solution.py:307
  81.2 0.0 collective-permute-done.10.refs_3_
  81.2 0.0 collective-permute-done.8.refs_2_
  81.3 1.2 %widen.7 = f32[1280,1280]{1,0:T(8,128)} custom-call(s32[1]{0:T(128)} %bitcast.refs_0_, s32[1]{0:T(128)} %bitcast.1.refs_1_, bf16[200,8,128]{2,1,0:T(8,128)(2,1)S(1)} %collective-permute-done.8.refs_2_, bf16[200,8,128]{2,1,0:T(8,128)(2,1)S(1)} %collective-permute-done.10.refs_3_, f32[1280,1280]{1,0:T(8,128)} %widen.6.refs_4_), custom_call_target="tpu_custom_call", output_to_operand_aliasing={{}: (4, {})} | custom-call | flops 1073741824 | bytes 1048576 | tf_op jit(solution)/shard_map/widen/pallas_call | solution.py:307
  (1 shorter events, 0.0 us)
Async XLA Ops:
  11.4 2.8 %collective-permute-start.5 = (bf16[160,1280]{1,0:T(8,128)(2,1)S(1)}, bf16[160,1280]{1,0:T(8,128)(2,1)S(1)}, u32[]{:S(2)}, u32[]{:S(2)}) collective-permute-start(bf16[160,1280]{1,0:T(8,128)(2,1)S(1)} %get-tuple-element.14), channel_id=1, source_target_pairs={{0,32},{32,0},{1,33},{33,1},{2,34},{34,2},{3,35},{35,3},{4,36},{36... | collective-permute-start | bytes 1228808 | tf_op jit(solution)/shard_map/ppermute | solution.py:324
  12.8 2.9 %collective-permute-start.3 = (bf16[160,1280]{1,0:T(8,128)(2,1)S(1)}, bf16[160,1280]{1,0:T(8,128)(2,1)S(1)}, u32[]{:S(2)}, u32[]{:S(2)}) collective-permute-start(bf16[160,1280]{1,0:T(8,128)(2,1)S(1)} %get-tuple-element.13), channel_id=1, source_target_pairs={{0,32},{32,0},{1,33},{33,1},{2,34},{34,2},{3,35},{35,3},{4,36},{36... | collective-permute-start | bytes 1228808 | tf_op jit(solution)/shard_map/ppermute | solution.py:324
  12.9 4.9 %collective-permute-start.1 = (bf16[160,1280]{1,0:T(8,128)(2,1)S(1)}, bf16[160,1280]{1,0:T(8,128)(2,1)S(1)}, u32[]{:S(2)}, u32[]{:S(2)}) collective-permute-start(bf16[160,1280]{1,0:T(8,128)(2,1)S(1)} %get-tuple-element.12), channel_id=1, source_target_pairs={{0,32},{32,0},{1,33},{33,1},{2,34},{34,2},{3,35},{35,3},{4,36},{36... | collective-permute-start | bytes 1228808 | tf_op jit(solution)/shard_map/ppermute | solution.py:324
  13.3 5.4 %collective-permute-start = (bf16[160,1280]{1,0:T(8,128)(2,1)S(1)}, bf16[160,1280]{1,0:T(8,128)(2,1)S(1)}, u32[]{:S(2)}, u32[]{:S(2)}) collective-permute-start(bf16[160,1280]{1,0:T(8,128)(2,1)S(1)} %get-tuple-element.11), channel_id=1, source_target_pairs={{0,32},{32,0},{1,33},{33,1},{2,34},{34,2},{3,35},{35,3},{4,36},{36... | collective-permute-start | bytes 1228808 | tf_op jit(solution)/shard_map/ppermute | solution.py:324
  14.3 7.2 %collective-permute-start.6 = (bf16[160,1280]{1,0:T(8,128)(2,1)S(1)}, bf16[160,1280]{1,0:T(8,128)(2,1)S(1)}, u32[]{:S(2)}, u32[]{:S(2)}) collective-permute-start(bf16[160,1280]{1,0:T(8,128)(2,1)S(1)} %shard_map.49), channel_id=1, source_target_pairs={{0,1},{4,5},{8,9},{12,13},{16,17},{20,21},{24,25},{28,29},{64,65},... | collective-permute-start | bytes 1228808 | tf_op jit(solution)/shard_map/ppermute | solution.py:348
  15.8 12.8 %collective-permute-start.4 = (bf16[160,1280]{1,0:T(8,128)(2,1)S(1)}, bf16[160,1280]{1,0:T(8,128)(2,1)S(1)}, u32[]{:S(2)}, u32[]{:S(2)}) collective-permute-start(bf16[160,1280]{1,0:T(8,128)(2,1)S(1)} %shard_map.48), channel_id=1, source_target_pairs={{0,3},{4,7},{8,11},{12,15},{16,19},{20,23},{24,27},{28,31},{64,67}... | collective-permute-start | bytes 1228808 | tf_op jit(solution)/shard_map/ppermute | solution.py:348
  17.9 10.7 %collective-permute-start.2 = (bf16[160,1280]{1,0:T(8,128)(2,1)S(1)}, bf16[160,1280]{1,0:T(8,128)(2,1)S(1)}, u32[]{:S(2)}, u32[]{:S(2)}) collective-permute-start(bf16[160,1280]{1,0:T(8,128)(2,1)S(1)} %shard_map.47), channel_id=1, source_target_pairs={{0,2},{4,6},{8,10},{12,14},{16,18},{20,22},{24,26},{28,30},{64,66}... | collective-permute-start | bytes 1228808 | tf_op jit(solution)/shard_map/ppermute | solution.py:348
  56.4 8.6 %collective-permute-start.11 = (bf16[200,8,128]{2,1,0:T(8,128)(2,1)S(1)}, bf16[200,8,128]{2,1,0:T(8,128)(2,1)S(1)}, u32[]{:S(2)}, u32[]{:S(2)}) collective-permute-start(bf16[200,8,128]{2,1,0:T(8,128)(2,1)S(1)} %slice.4.refs_2_), channel_id=1, source_target_pairs={{1,0},{5,4},{9,8},{13,12},{17,16},{21,20},{25,24},{29,28},{65,64},... | collective-permute-start | bytes 1228808 | tf_op jit(solution)/shard_map/ppermute | solution.py:356
  56.5 13.2 %collective-permute-start.9 = (bf16[200,8,128]{2,1,0:T(8,128)(2,1)S(1)}, bf16[200,8,128]{2,1,0:T(8,128)(2,1)S(1)}, u32[]{:S(2)}, u32[]{:S(2)}) collective-permute-start(bf16[200,8,128]{2,1,0:T(8,128)(2,1)S(1)} %slice.4.refs_2_), channel_id=1, source_target_pairs={{2,0},{6,4},{10,8},{14,12},{18,16},{22,20},{26,24},{30,28},{66,64}... | collective-permute-start | bytes 1228808 | tf_op jit(solution)/shard_map/ppermute | solution.py:356
  59.7 14.7 %collective-permute-start.7 = (bf16[200,8,128]{2,1,0:T(8,128)(2,1)S(1)}, bf16[200,8,128]{2,1,0:T(8,128)(2,1)S(1)}, u32[]{:S(2)}, u32[]{:S(2)}) collective-permute-start(bf16[200,8,128]{2,1,0:T(8,128)(2,1)S(1)} %slice.4.refs_2_), channel_id=1, source_target_pairs={{3,0},{7,4},{11,8},{15,12},{19,16},{23,20},{27,24},{31,28},{67,64}... | collective-permute-start | bytes 1228808 | tf_op jit(solution)/shard_map/ppermute | solution.py:356
  60.4 17.2 %collective-permute-start.13 = (bf16[200,8,128]{2,1,0:T(8,128)(2,1)S(1)}, bf16[200,8,128]{2,1,0:T(8,128)(2,1)S(1)}, u32[]{:S(2)}, u32[]{:S(2)}) collective-permute-start(bf16[200,8,128]{2,1,0:T(8,128)(2,1)S(1)} %slice.4.refs_2_), channel_id=1, source_target_pairs={{0,32},{32,0},{1,33},{33,1},{2,34},{34,2},{3,35},{35,3},{4,36},{36... | collective-permute-start | bytes 1228808 | tf_op jit(solution)/shard_map/ppermute | solution.py:324
  65.0 13.8 %collective-permute-start.12 = (bf16[200,8,128]{2,1,0:T(8,128)(2,1)S(1)}, bf16[200,8,128]{2,1,0:T(8,128)(2,1)S(1)}, u32[]{:S(2)}, u32[]{:S(2)}) collective-permute-start(bf16[200,8,128]{2,1,0:T(8,128)(2,1)S(1)} %collective-permute-done.11.refs_2_), channel_id=1, source_target_pairs={{0,32},{32,0},{1,33},{33,1},{2,34},{34,2},{3,35},{35,3},{4,36},{36... | collective-permute-start | bytes 1228808 | tf_op jit(solution)/shard_map/ppermute | solution.py:324
  69.8 11.5 %collective-permute-start.10 = (bf16[200,8,128]{2,1,0:T(8,128)(2,1)S(1)}, bf16[200,8,128]{2,1,0:T(8,128)(2,1)S(1)}, u32[]{:S(2)}, u32[]{:S(2)}) collective-permute-start(bf16[200,8,128]{2,1,0:T(8,128)(2,1)S(1)} %collective-permute-done.9.refs_3_), channel_id=1, source_target_pairs={{0,32},{32,0},{1,33},{33,1},{2,34},{34,2},{3,35},{35,3},{4,36},{36... | collective-permute-start | bytes 1228808 | tf_op jit(solution)/shard_map/ppermute | solution.py:324
  74.4 6.9 %collective-permute-start.8 = (bf16[200,8,128]{2,1,0:T(8,128)(2,1)S(1)}, bf16[200,8,128]{2,1,0:T(8,128)(2,1)S(1)}, u32[]{:S(2)}, u32[]{:S(2)}) collective-permute-start(bf16[200,8,128]{2,1,0:T(8,128)(2,1)S(1)} %collective-permute-done.7.refs_2_), channel_id=1, source_target_pairs={{0,32},{32,0},{1,33},{33,1},{2,34},{34,2},{3,35},{35,3},{4,36},{36... | collective-permute-start | bytes 1228808 | tf_op jit(solution)/shard_map/ppermute | solution.py:324
